TPU v7x, 64 devices: a 2x2x8 block of a 4x4x8 slice. The times are simulated.
64 devices in a mesh: dp: 4 (over x, y), fsdp: 16 (over z, core).
Axes of the slice: x: 2, y: 2, z: 8, core: 2. Of those that a mesh axis runs over, the one named last changes fastest.
The devices are a block of a 4x4x8 slice.
Arguments:
- hidden: bfloat16 [512, 128, 1024], P(('dp', 'fsdp')), parts along dimension 0
- doc_lens: int32 [512], P(('dp', 'fsdp')), parts along dimension 0
- ln_par: float32 [2, 4, 1024], P(None, None, 'fsdp')
- w_qkv: bfloat16 [2, 1024, 16, 192], P(None, 'fsdp')
- b_qkv: bfloat16 [2, 3072], P(None, 'fsdp')
- w_out: bfloat16 [2, 1024, 1024], P(None, 'fsdp')
- b_out: bfloat16 [2, 1024], P(None, 'fsdp')
- w_up: bfloat16 [2, 1024, 4096], P(None, 'fsdp')
- b_up: bfloat16 [2, 4096], P(None, 'fsdp')
- w_down: bfloat16 [2, 4096, 1024], P(None, 'fsdp')
- b_down: bfloat16 [2, 1024], P(None, 'fsdp')
Outputs:
- output: bfloat16 [512, 128, 1024], P(('dp', 'fsdp')), parts along dimension 0
There are 4 independent parts. A program takes and returns all parts, laid end to end along the dimension named above; an argument that names none is the same for every part.
All inputs are finite; a program needn't handle non-finite values.
Results may differ from a plain program's by a relative error of at most 0.00929409.
Values are sent between devices in bfloat16 or wider.
A program may use at most 768 MiB of HBM per device.

v0:
```python
import jax
import jax.numpy as jnp
from jax import lax
from jax.sharding import PartitionSpec as P

ROPE_BASE = 10000.0
LN_EPS = 1e-5


def layer_norm(row_vals, gain_vec, shift_vec):
    mean_vals = jnp.mean(row_vals, axis=-1, keepdims=True)
    centered = row_vals - mean_vals
    var_vals = jnp.mean(centered * centered, axis=-1, keepdims=True)
    normed = centered * lax.rsqrt(var_vals + LN_EPS)
    return (normed * gain_vec + shift_vec).astype(jnp.bfloat16)


def rotary_tables(seq_len, rot_dim):
    inv_freq = 1.0 / (ROPE_BASE ** (jnp.arange(0, rot_dim, 2, dtype=jnp.float32) / rot_dim))
    angles = jnp.arange(seq_len, dtype=jnp.float32)[:, None] * inv_freq[None, :]
    angles = jnp.concatenate([angles, angles], axis=-1)
    return jnp.cos(angles), jnp.sin(angles)


def apply_rotary(head_vals, cos_tab, sin_tab):
    rot_dim = cos_tab.shape[-1]
    half_rot = rot_dim // 2
    rot_part = head_vals[..., :rot_dim].astype(jnp.float32)
    turned = jnp.concatenate([-rot_part[..., half_rot:], rot_part[..., :half_rot]], axis=-1)
    rotated = rot_part * cos_tab[:, None, :] + turned * sin_tab[:, None, :]
    return jnp.concatenate([rotated.astype(jnp.bfloat16), head_vals[..., rot_dim:]], axis=-1)


def attention_core(qkv_heads, lens_loc):
    num_docs, seq_len, num_heads, triple = qkv_heads.shape
    head_dim = triple // 3
    cos_tab, sin_tab = rotary_tables(seq_len, head_dim // 4)
    queries = apply_rotary(qkv_heads[..., :head_dim], cos_tab, sin_tab)
    keys_rot = apply_rotary(qkv_heads[..., head_dim:2 * head_dim], cos_tab, sin_tab)
    values = qkv_heads[..., 2 * head_dim:]
    scores = jnp.einsum('nqhe,nkhe->nhqk', queries, keys_rot, preferred_element_type=jnp.float32) * (head_dim ** -0.5)
    positions = jnp.arange(seq_len)
    causal = positions[None, :] <= positions[:, None]
    visible = causal[None, None] & (positions[None, None, None, :] < lens_loc[:, None, None, None])
    prob_bf = jax.nn.softmax(jnp.where(visible, scores, -1e30), axis=-1).astype(jnp.bfloat16)
    context = jnp.einsum('nhqk,nkhe->nqhe', prob_bf, values, preferred_element_type=jnp.float32)
    return context.astype(jnp.bfloat16).reshape(num_docs * seq_len, num_heads * head_dim)


def layer_forward(x_loc, lens_loc, ln_full, w_qkv_full, b_qkv_full, w_out_full, b_out_full, w_up_full, b_up_full, w_down_full, b_down_full):
    num_docs, seq_len, d_model = x_loc.shape
    x_rows = x_loc.reshape(num_docs * seq_len, d_model).astype(jnp.float32)
    attn_in = layer_norm(x_rows, ln_full[0], ln_full[1])
    mlp_in = layer_norm(x_rows, ln_full[2], ln_full[3])
    qkv_rows = jnp.dot(attn_in, w_qkv_full.reshape(d_model, -1), preferred_element_type=jnp.float32) + b_qkv_full.astype(jnp.float32)
    qkv_heads = qkv_rows.astype(jnp.bfloat16).reshape(num_docs, seq_len, w_qkv_full.shape[1], w_qkv_full.shape[2])
    context = attention_core(qkv_heads, lens_loc)
    attn_out = jnp.dot(context, w_out_full, preferred_element_type=jnp.float32) + b_out_full.astype(jnp.float32)
    up_rows = jnp.dot(mlp_in, w_up_full, preferred_element_type=jnp.float32) + b_up_full.astype(jnp.float32)
    act_rows = jax.nn.gelu(up_rows, approximate=False).astype(jnp.bfloat16)
    mlp_out = jnp.dot(act_rows, w_down_full, preferred_element_type=jnp.float32) + b_down_full.astype(jnp.float32)
    return (x_rows + attn_out + mlp_out).astype(jnp.bfloat16).reshape(num_docs, seq_len, d_model)


def gather_full(piece, axis_idx):
    return lax.all_gather(piece, 'fsdp', axis=axis_idx, tiled=True)


def solution(mesh):
    row_spec = P(('dp', 'fsdp'), None, None)
    in_specs = (row_spec, P(('dp', 'fsdp')), P(None, None, 'fsdp'), P(None, 'fsdp', None, None), P(None, 'fsdp'), P(None, 'fsdp', None), P(None, 'fsdp'), P(None, 'fsdp', None), P(None, 'fsdp'), P(None, 'fsdp', None), P(None, 'fsdp'))

    def local_step(hidden_loc, lens_loc, ln_par, w_qkv, b_qkv, w_out, b_out, w_up, b_up, w_down, b_down):
        x_loc = hidden_loc
        for layer_idx in range(ln_par.shape[0]):
            ln_full = gather_full(ln_par[layer_idx], 1)
            w_qkv_full = gather_full(w_qkv[layer_idx], 0)
            b_qkv_full = gather_full(b_qkv[layer_idx], 0)
            w_out_full = gather_full(w_out[layer_idx], 0)
            b_out_full = gather_full(b_out[layer_idx], 0)
            w_up_full = gather_full(w_up[layer_idx], 0)
            b_up_full = gather_full(b_up[layer_idx], 0)
            w_down_full = gather_full(w_down[layer_idx], 0)
            b_down_full = gather_full(b_down[layer_idx], 0)
            x_loc = layer_forward(x_loc, lens_loc, ln_full, w_qkv_full, b_qkv_full, w_out_full, b_out_full, w_up_full, b_up_full, w_down_full, b_down_full)
        return x_loc

    return jax.shard_map(local_step, mesh=mesh, in_specs=in_specs, out_specs=row_spec, check_vma=False)
```

profile of v0, /device:TPU:21, one launch (start us, length us, event | category | flops | bytes accessed | tf_op | source)
XLA Modules:
  0.0 529.2 jit_solution(2969780606187020650)
XLA Ops:
  22.1 53.1 %all-reduce.6 = (bf16[3072]{0:T(1024)(128)(2,1)S(1)}, bf16[1024]{0:T(1024)(128)(2,1)S(1)}, bf16[1024]{0:T(1024)(128)(2,1)S(1)}, bf16[3072]{0:T(1024)(128)(2,1)S(...) all-reduce(bf16[3072]{0:T(1024)(128)(2,1)S(1)} %dynamic-update-slic, ...), channel_id=4, replica_groups=mesh['dp'=4,'fsdp'=16] {'fsdp'}, use_global_device_ids=true, to_apply=%add | all-reduce | flops 10240 | bytes 40960
  75.9 22.3 %all-gather = f32[1,4,1024]{1,0,2:T(1,128)S(1)} all-gather(f32[1,4,64]{1,0,2:T(1,128)S(1)} %copy.87), channel_id=2, replica_groups=mesh['dp'=4,'fsdp'=16] {'fsdp'}, dimensions={2}, use_global_device_ids=true | all-gather | bytes 17408 | tf_op jit(solution)/shard_map/all_gather | solution.py:66
  98.3 21.7 %slice_reduce_fusion.5 = (f32[1024]{0:T(1024)S(1)}, f32[1024]{0:T(1024)S(1)}, f32[1024]{0:T(1024)S(1)}, f32[1024]{0:T(1024)S(1)}) fusion(f32[1,4,1024]{1,0,2:T(1,128)S(1)} %all-gather), kind=kLoop, calls=%fused_computation.149 | loop fusion | bytes 32768 | tf_op jit(solution)/shard_map/slice | solution.py:54
  121.9 15.6 %all-gather.6 = bf16[1,4096]{1,0:T(2,128)(2,1)S(1)} all-gather(bf16[1,256]{1,0:T(2,128)(2,1)S(1)} %get-tuple-element.50), channel_id=8, replica_groups=mesh['dp'=4,'fsdp'=16] {'fsdp'}, dimensions={1}, use_global_device_ids=true | all-gather | bytes 8704 | tf_op jit(solution)/shard_map/all_gather | solution.py:66
  138.2 18.5 %all-gather.9 = f32[1,4,1024]{1,0,2:T(1,128)S(1)} all-gather(f32[1,4,64]{1,0,2:T(1,128)S(1)} %copy.94), channel_id=11, replica_groups=mesh['dp'=4,'fsdp'=16] {'fsdp'}, dimensions={2}, use_global_device_ids=true | all-gather | bytes 17408 | tf_op jit(solution)/shard_map/all_gather | solution.py:66
  156.7 22.1 %slice_reduce_fusion.1 = (f32[1024]{0:T(1024)}, f32[1024]{0:T(1024)}, f32[1024]{0:T(1024)}, f32[1024]{0:T(1024)}) fusion(f32[1,4,1024]{1,0,2:T(1,128)S(1)} %all-gather.9), kind=kLoop, calls=%fused_computation.143 | loop fusion | bytes 32768 | tf_op jit(solution)/shard_map/slice | solution.py:54
  180.0 14.7 %all-gather.15 = bf16[1,4096]{1,0:T(2,128)(2,1)S(1)} all-gather(bf16[1,256]{1,0:T(2,128)(2,1)S(1)} %get-tuple-element.49), channel_id=17, replica_groups=mesh['dp'=4,'fsdp'=16] {'fsdp'}, dimensions={1}, use_global_device_ids=true | all-gather | bytes 8704 | tf_op jit(solution)/shard_map/all_gather | solution.py:66
  199.8 12.1 %copy.61 = bf16[1,1024,16,192]{1,3,2,0:T(8,128)(2,1)} copy(bf16[1,1024,16,192]{3,2,0,1:T(8,128)(2,1)} %all-gather.27.cloned.1.call-done) | data formatting | bytes 12582912 | tf_op jit(solution)/shard_map/all_gather | solution.py:66
  211.9 11.3 %add_convert_fusion.1 = bf16[1024,3072]{1,0:T(8,128)(2,1)} fusion(f32[3072]{0:T(1024)S(1)} %convert_element_type.159, bf16[1024,1024]{1,0:T(8,128)(2,1)S(1)} %bitcast.116, bf16[1024,3072]{0,1:T(8,128)(2,1)} %bitcast.115), kind=kOutput, calls=%fused_computation.41 | convolution fusion | flops 6448742400 | bytes 14692352 | tf_op jit(solution)/shard_map/dot_general | solution.py:55
  223.3 14.6 %reshape.279 = bf16[8,128,16,192]{3,2,1,0:T(8,128)(2,1)} reshape(bf16[1024,3072]{1,0:T(8,128)(2,1)} %add_convert_fusion.1) | data formatting | bytes 12582912 | tf_op jit(solution)/shard_map/reshape | solution.py:56
  237.9 7.7 %fusion.211 = (bf16[8,128,16,48]{3,2,1,0:T(8,128)(2,1)}, bf16[8,128,16,48]{3,2,1,0:T(8,128)(2,1)}) fusion(bf16[8,128,16,192]{3,2,1,0:T(8,128)(2,1)} %reshape.279), kind=kLoop, calls=%fused_computation.245 | loop fusion | bytes 6291456 | tf_op jit(solution)/shard_map/slice | solution.py:31
  250.7 4.7 copy.92
  256.6 4.7 copy.90
  263.3 4.8 copy.91
  268.2 5.8 %copy.93 = bf16[8,128,16,48]{1,3,2,0:T(8,128)(2,1)} copy(bf16[8,128,16,48]{3,2,1,0:T(8,128)(2,1)} %get-tuple-element.27) | data formatting | bytes 3145728
  283.8 4.8 convert_bitcast_fusion.1
  290.4 11.8 %copy.72 = bf16[1,1024,16,192]{1,3,2,0:T(8,128)(2,1)} copy(bf16[1,1024,16,192]{3,2,0,1:T(8,128)(2,1)} %all-gather.35.cloned.1.call-done) | data formatting | bytes 12582912 | tf_op jit(solution)/shard_map/all_gather | solution.py:66
  302.2 5.9 %fusion.81 = f32[1024,1024]{1,0:T(8,128)} fusion(bf16[128,8,8,128]{3,2,1,0:T(8,128)(2,1)S(1)} %bitcast.112, bf16[1,1024,1024]{2,1,0:T(8,128)(2,1)} %all-gather.29.cloned.1.call-done), kind=kOutput, calls=%fused_computation.101 | convolution fusion | flops 2147483648 | bytes 8388608 | tf_op jit(solution)/shard_map/dot_general | solution.py:58
  308.1 48.2 %fusion.117.clone.4 = bf16[1024,4096]{1,0:T(8,128)(2,1)} fusion(f32[4096]{0:T(1024)S(1)} %bitcast.118, bf16[1024,1024]{1,0:T(8,128)(2,1)} %fusion.68, bf16[1,1024,4096]{2,1,0:T(8,128)(2,1)} %all-gather.31.cloned.1.call-done), kind=kOutput, calls=%fused_computation.6.clone.clone.clone.clone.clone.clone.1 | convolution fusion | flops 8866758656 | bytes 18890752 | tf_op jit(solution)/shard_map/dot_general | solution.py:59
  356.4 14.7 %convert_reduce_fusion = (f32[1024]{0:T(1024)S(1)}, bf16[1024,1024]{1,0:T(8,128)(2,1)S(1)}) fusion(f32[1024]{0:T(1024)S(1)} %copy-done.22, bf16[1,4096,1024]{2,1,0:T(8,128)(2,1)} %all-gather.33.cloned.1.call-done, f32[1024,1024]{1,0:T(8,128)} %fusion.81, f32[1024]{0:T(1024)S(1)} %copy-done.23, bf16[8,128,1024]{2,1,0:T(8,128)(2,1)S(1)} %copy-done.3, ...), kind=kOutput, calls=%fused_computation.60 | convolution fusion | flops 8598322176 | bytes 25178112 | tf_op jit(solution)/shard_map/dot_general | solution.py:61
  372.4 9.0 %add_convert_fusion = bf16[1024,3072]{1,0:T(8,128)(2,1)} fusion(f32[3072]{0:T(1024)S(1)} %copy-done.15, bf16[1024,3072]{0,1:T(8,128)(2,1)S(1)} %bitcast.114, bf16[1024,1024]{1,0:T(8,128)(2,1)S(1)} %get-tuple-element.58, f32[1024]{0:T(1024)S(1)} %copy-done.18, f32[1024]{0:T(1024)S(1)} %copy-done.19, f32[1024]{0:T(1024)S(1)} %add_rsqrt_fusion, ...), kind=kOutput, calls=%fused_computation.40 | convolution fusion | flops 6455033856 | bytes 14708736 | tf_op jit(solution)/shard_map/dot_general | solution.py:55
  381.5 14.7 %reshape.280 = bf16[8,128,16,192]{3,2,1,0:T(8,128)(2,1)} reshape(bf16[1024,3072]{1,0:T(8,128)(2,1)} %add_convert_fusion) | data formatting | bytes 12582912 | tf_op jit(solution)/shard_map/reshape | solution.py:56
  396.1 7.7 %fusion.209 = (bf16[8,128,16,48]{3,2,1,0:T(8,128)(2,1)}, bf16[8,128,16,48]{3,2,1,0:T(8,128)(2,1)}) fusion(bf16[8,128,16,192]{3,2,1,0:T(8,128)(2,1)} %reshape.280), kind=kLoop, calls=%fused_computation.243 | loop fusion | bytes 6291456 | tf_op jit(solution)/shard_map/slice | solution.py:31
  409.1 4.7 copy.99
  415.0 4.7 copy.97
  421.7 4.9 copy.98
  428.5 5.7 %copy.100 = bf16[8,128,16,48]{1,3,2,0:T(8,128)(2,1)} copy(bf16[8,128,16,48]{3,2,1,0:T(8,128)(2,1)} %get-tuple-element.23) | data formatting | bytes 3145728
  439.6 4.5 fusion.220
  444.1 4.8 convert_bitcast_fusion
  450.7 6.0 %fusion.78 = f32[1024,1024]{1,0:T(8,128)} fusion(bf16[128,8,8,128]{3,2,1,0:T(8,128)(2,1)S(1)} %bitcast.113, bf16[1,1024,1024]{2,1,0:T(8,128)(2,1)} %all-gather.37.cloned.1.call-done), kind=kOutput, calls=%fused_computation.98 | convolution fusion | flops 2147483648 | bytes 8388608 | tf_op jit(solution)/shard_map/dot_general | solution.py:58
  456.7 49.4 %fusion.241 = bf16[1024,4096]{1,0:T(8,128)(2,1)} fusion(f32[4096]{0:T(1024)S(1)} %bitcast.117, bf16[1,1024,4096]{2,1,0:T(8,128)(2,1)} %all-gather.39.cloned.1.call-done, bf16[1024,1024]{1,0:T(8,128)(2,1)} %copy-done.5, f32[1024]{0:T(1024)S(1)} %copy-done.17, f32[1024]{0:T(1024)S(1)} %copy-done.16, f32[1024]{0:T(1024)S(1)} %add_rsqrt_fusion, ...), kind=kOutput, calls=%fused_computation.9.clone.clone.clone.clone.1 | convolution fusion | flops 8873050112 | bytes 18907136 | tf_op jit(solution)/shard_map/dot_general | solution.py:59
  506.1 15.7 %fusion.52 = bf16[1024,1024]{1,0:T(8,128)(2,1)} fusion(bf16[1024,1024]{1,0:T(8,128)(2,1)S(1)} %copy-done.6, f32[1024,1024]{1,0:T(8,128)} %fusion.78, f32[1024]{0:T(1024)S(1)} %copy-done.20, f32[1024]{0:T(1024)S(1)} %copy-done.21, bf16[1,4096,1024]{2,1,0:T(8,128)(2,1)} %all-gather.41.cloned.1.call-done, bf16[1024,4096]{1,0:T(8,128)(2,1)} %fusion.241), kind=kOutput, calls=%fused_computation.71 | convolution fusion | flops 8596226048 | bytes 25174016 | tf_op jit(solution)/shard_map/dot_general | solution.py:61
  (157 shorter events, 62.3 us)
Async XLA Ops:
  6.5 12.4 %copy-start.30 = (u32[64]{0:T(128)S(1)}, u32[64]{0:T(128)}, u32[]{:S(2)}) copy-start(u32[64]{0:T(128)} %constant.87) | copy-start | bytes 772
  6.5 12.3 %copy-start.24 = (bf16[2,192]{1,0:T(2,128)(2,1)S(1)}, bf16[2,192]{1,0:T(2,128)(2,1)}, u32[]{:S(2)}) copy-start(bf16[2,192]{1,0:T(2,128)(2,1)} %param.15) | copy-start | bytes 2308
  6.6 12.3 %copy-start.27 = (bf16[2,64]{1,0:T(2,128)(2,1)S(1)}, bf16[2,64]{1,0:T(2,128)(2,1)}, u32[]{:S(2)}) copy-start(bf16[2,64]{1,0:T(2,128)(2,1)} %param.21) | copy-start | bytes 772
  6.6 14.3 %copy-start.28 = (bf16[2,64]{1,0:T(2,128)(2,1)S(1)}, bf16[2,64]{1,0:T(2,128)(2,1)}, u32[]{:S(2)}) copy-start(bf16[2,64]{1,0:T(2,128)(2,1)} %param.17) | copy-start | bytes 772
  6.6 69.3 %copy-start.25 = (f32[2,4,64]{2,1,0:T(4,128)S(1)}, f32[2,4,64]{2,1,0:T(4,128)}, u32[]{:S(2)}) copy-start(f32[2,4,64]{2,1,0:T(4,128)} %param.13) | copy-start | bytes 6148
  6.6 113.4 %copy-start.2 = (bf16[8,128,1024]{2,1,0:T(8,128)(2,1)S(1)}, bf16[8,128,1024]{2,1,0:T(8,128)(2,1)}, u32[]{:S(2)}) copy-start(bf16[8,128,1024]{2,1,0:T(8,128)(2,1)} %param.11) | copy-start | bytes 6291460
  6.6 114.6 %copy-start.29 = (s32[8]{0:T(128)S(1)}, s32[8]{0:T(128)}, u32[]{:S(2)}) copy-start(s32[8]{0:T(128)} %param.12) | copy-start | bytes 100
  6.6 115.3 %copy-start.26 = (bf16[2,256]{1,0:T(2,128)(2,1)S(1)}, bf16[2,256]{1,0:T(2,128)(2,1)}, u32[]{:S(2)}) copy-start(bf16[2,256]{1,0:T(2,128)(2,1)} %param.19) | copy-start | bytes 3076
  6.6 193.2 %all-gather.27.cloned.1.call-start = ((), (), s32[]{:S(2)}) async-start(), calls=%async_computation | async-start | bytes 8912896 | tf_op jit(solution)/shard_map/all_gather | solution.py:66
  9.1 281.3 %all-gather.35.cloned.1.call-start = ((), (), s32[]{:S(2)}) async-start(), calls=%async_computation.4 | async-start | bytes 8912896 | tf_op jit(solution)/shard_map/all_gather | solution.py:66
  9.9 292.3 %all-gather.29.cloned.1.call-start = ((), (), s32[]{:S(2)}) async-start(), calls=%async_computation.1 | async-start | bytes 2228224 | tf_op jit(solution)/shard_map/all_gather | solution.py:66
  11.7 296.4 %all-gather.31.cloned.1.call-start = ((), (), s32[]{:S(2)}) async-start(), calls=%async_computation.2 | async-start | bytes 8912896 | tf_op jit(solution)/shard_map/all_gather | solution.py:66
  14.2 342.2 %all-gather.33.cloned.1.call-start = ((), (), s32[]{:S(2)}) async-start(), calls=%async_computation.3 | async-start | bytes 8912896 | tf_op jit(solution)/shard_map/all_gather | solution.py:66
  16.5 434.1 %all-gather.37.cloned.1.call-start = ((), (), s32[]{:S(2)}) async-start(), calls=%async_computation.5 | async-start | bytes 2228224 | tf_op jit(solution)/shard_map/all_gather | solution.py:66
  17.2 439.5 %all-gather.39.cloned.1.call-start = ((), (), s32[]{:S(2)}) async-start(), calls=%async_computation.6 | async-start | bytes 8912896 | tf_op jit(solution)/shard_map/all_gather | solution.py:66
  18.0 488.1 %all-gather.41.cloned.1.call-start = ((), (), s32[]{:S(2)}) async-start(), calls=%async_computation.7 | async-start | bytes 8912896 | tf_op jit(solution)/shard_map/all_gather | solution.py:66
  121.2 154.1 %copy-start.10 = (f32[128,16]{0,1:T(8,128)}, f32[128,16]{0,1:T(8,128)S(1)}, u32[]{:S(2)}) copy-start(f32[128,16]{0,1:T(8,128)S(1)} %get-tuple-element.47) | copy-start | bytes 24580
  121.2 154.1 %copy-start.12 = (f32[128,16]{0,1:T(8,128)}, f32[128,16]{0,1:T(8,128)S(1)}, u32[]{:S(2)}) copy-start(f32[128,16]{0,1:T(8,128)S(1)} %get-tuple-element.48) | copy-start | bytes 24580
  195.5 84.0 %copy-start.8 = (pred[8,128,128]{1,2,0:T(8,128)(4,1)}, pred[8,128,128]{1,2,0:T(8,128)(4,1)S(1)}, u32[]{:S(2)}) copy-start(pred[8,128,128]{1,2,0:T(8,128)(4,1)S(1)} %broadcast_and_fusion) | copy-start | bytes 393220
  199.8 12.1 %copy-start.7 = (bf16[8,128,1024]{2,1,0:T(8,128)(2,1)S(1)}, bf16[8,128,1024]{2,1,0:T(8,128)(2,1)}, u32[]{:S(2)}) copy-start(bf16[8,128,1024]{2,1,0:T(8,128)(2,1)} %fusion.62) | copy-start | bytes 6291460
  308.1 48.2 %copy-start.3 = (bf16[8,128,1024]{2,1,0:T(8,128)(2,1)S(1)}, bf16[8,128,1024]{2,1,0:T(8,128)(2,1)}, u32[]{:S(2)}) copy-start(bf16[8,128,1024]{2,1,0:T(8,128)(2,1)} %param.11) | copy-start | bytes 6291460
  308.1 48.2 %copy-start.22 = (f32[1024]{0:T(1024)S(1)}, f32[1024]{0:T(1024)}, u32[]{:S(2)}) copy-start(f32[1024]{0:T(1024)} %convert_element_type.161) | copy-start | bytes 12292
  308.1 48.2 %copy-start.23 = (f32[1024]{0:T(1024)S(1)}, f32[1024]{0:T(1024)}, u32[]{:S(2)}) copy-start(f32[1024]{0:T(1024)} %convert_element_type.160) | copy-start | bytes 12292
  356.3 16.1 %copy-start.15 = (f32[3072]{0:T(1024)S(1)}, f32[3072]{0:T(1024)}, u32[]{:S(2)}) copy-start(f32[3072]{0:T(1024)} %convert_element_type.162) | copy-start | bytes 36868
  356.3 16.1 %copy-start.18 = (f32[1024]{0:T(1024)S(1)}, f32[1024]{0:T(1024)}, u32[]{:S(2)}) copy-start(f32[1024]{0:T(1024)} %get-tuple-element.6) | copy-start | bytes 12292
  356.3 16.1 %copy-start.19 = (f32[1024]{0:T(1024)S(1)}, f32[1024]{0:T(1024)}, u32[]{:S(2)}) copy-start(f32[1024]{0:T(1024)} %get-tuple-element.7) | copy-start | bytes 12292
  356.4 16.1 %copy-start.4 = (bf16[1,1024,16,192]{1,3,2,0:T(8,128)(2,1)S(1)}, bf16[1,1024,16,192]{1,3,2,0:T(8,128)(2,1)}, u32[]{:S(2)}) copy-start(bf16[1,1024,16,192]{1,3,2,0:T(8,128)(2,1)} %copy.72) | copy-start | bytes 18874372
  421.7 13.5 %copy-start.11 = (f32[128,16]{0,1:T(8,128)S(1)}, f32[128,16]{0,1:T(8,128)}, u32[]{:S(2)}) copy-start(f32[128,16]{0,1:T(8,128)} %copy-done.10) | copy-start | bytes 24580
  421.7 13.5 %copy-start.13 = (f32[128,16]{0,1:T(8,128)S(1)}, f32[128,16]{0,1:T(8,128)}, u32[]{:S(2)}) copy-start(f32[128,16]{0,1:T(8,128)} %copy-done.12) | copy-start | bytes 24580
  456.7 49.4 %copy-start.6 = (bf16[1024,1024]{1,0:T(8,128)(2,1)S(1)}, bf16[1024,1024]{1,0:T(8,128)(2,1)}, u32[]{:S(2)}) copy-start(bf16[1024,1024]{1,0:T(8,128)(2,1)} %copy-done.5) | copy-start | bytes 6291460
  456.7 49.4 %copy-start.20 = (f32[1024]{0:T(1024)S(1)}, f32[1024]{0:T(1024)}, u32[]{:S(2)}) copy-start(f32[1024]{0:T(1024)} %convert_element_type.164) | copy-start | bytes 12292
  456.7 49.4 %copy-start.21 = (f32[1024]{0:T(1024)S(1)}, f32[1024]{0:T(1024)}, u32[]{:S(2)}) copy-start(f32[1024]{0:T(1024)} %convert_element_type.163) | copy-start | bytes 12292
  (9 other events, 55.4 us)
Sparse Core Ops, SparseCore 0:
  9.2 57.9 all-gather.26
  68.9 53.9 all-gather.34
  124.5 34.6 all-gather.28
  160.6 51.3 all-gather.30
  213.5 51.0 all-gather.32
  266.0 34.7 all-gather.36
  302.5 51.0 all-gather.38
  355.2 51.0 all-gather.40
where the time goes:
time: 540 us; the launch traced here: 529 us
  local copies, waits for them, and re-layouts  180 us (33%)
  matrix products  175 us (32%)
  blocking collectives  124 us (23%)
  other arithmetic  30.5 us (6%)
  between operations  15.9 us (3%)
    dot_general x2, matrix products, layer_forward(): jnp.dot(mlp_in, w_up_full, preferred_element_type=jnp.float32)  97.5 us
    all_gather x4, blocking collectives, gather_full(): return lax.all_gather(piece, 'fsdp', axis=axis_idx, tiled=True)  71.1 us
    unnamed x1, blocking collectives  53.1 us
    unnamed x88, local copies, waits for them, and re-layouts  47.5 us
    slice x2, local copies, waits for them, and re-layouts, layer_forward(): mlp_in = layer_norm(x_rows, ln_full[2], ln_full[3])  43.8 us
    dot_general x2, matrix products, layer_forward(): jnp.dot(act_rows, w_down_full, preferred_element_type=jnp.float32)  30.4 us
    reshape x2, local copies, waits for them, and re-layouts, layer_forward(): qkv_rows.astype(jnp.bfloat16)  29.3 us
    all_gather x2, local copies, waits for them, and re-layouts, gather_full(): return lax.all_gather(piece, 'fsdp', axis=axis_idx, tiled=True)  24 us
  transfers between devices with their start and end apart: 8, of which 0 were waited for; matrix products, arithmetic and copies ran while one was open for 69% of the time, Pallas kernels for 0%

commit v1 on v0

v1 whole, which is shorter than its diff:
```python
import math

import jax
import jax.numpy as jnp
import numpy as np
from jax import lax
from jax.experimental import pallas as pl
from jax.experimental.pallas import tpu as pltpu
from jax.sharding import PartitionSpec as P

MESH = pl.DeviceIdType.MESH
ROPE_BASE = 10000.0
LN_EPS = 1e-5
BF = jnp.bfloat16
F32 = jnp.float32
TILE = 256
STEPS = 4
PAR_ROWS = 16


def rotary_lanes(seq_len, head_dim):
    rot = head_dim // 4
    half = rot // 2
    inv_freq = (1.0 / (ROPE_BASE ** (np.arange(0, rot, 2, dtype=np.float32) / rot))).astype(np.float32)
    angles = np.arange(seq_len, dtype=np.float32)[:, None] * inv_freq[None, :]
    cos_v, sin_v = np.cos(angles), np.sin(angles)
    tab = np.zeros((3, seq_len, 2 * head_dim), np.float32)
    tab[0] = 1.0
    for base in (0, head_dim):
        tab[0, :, base:base + half] = cos_v
        tab[0, :, base + half:base + rot] = cos_v
        tab[1, :, base:base + half] = -sin_v
        tab[2, :, base + half:base + rot] = sin_v
    return tab


def make_kernel(n_layers, n_z, side, docs, seq_len, d_model, n_heads, ff):
    head_dim = d_model // n_heads
    half_rot = head_dim // 8
    tokens = docs * seq_len
    lanes = 2 * head_dim
    wide_rows = d_model // (2 * n_z)
    down_rows = ff // (2 * n_z)
    n_qkv = 3 * d_model
    n_up0 = ff // 2
    far = n_z // 2

    stages = (
        ("w", 0, n_qkv, 0, wide_rows),
        ("w", n_qkv, d_model + n_up0, 0, wide_rows),
        ("w", n_qkv + d_model + n_up0, ff - n_up0, 0, wide_rows),
        ("d", 0, d_model, 0, down_rows // 2),
        ("d", 0, d_model, down_rows // 2, down_rows // 2),
    )
    per_layer = len(stages)

    def kernel(x_hbm, lens_ref, par_ref, rope_ref, wq_hbm, wo_hbm, wu_hbm, wd_hbm,
               out_hbm, gw, gd,
               x_s, a_s, m_s, q_s, k_s, v_s, ctx_s, act_a, act_b, acc_s,
               w_a, w_b, w_c, w_d0, w_d1, st_q, st_o, st_u, st_d,
               pg, tab, tab_up,
               z_send, c_send, d_send, z_recv, x_recv, y_recv, d_recv,
               p_zsend, p_dsend, p_zrecv, p_drecv,
               x_sem, st_sem, own_sem, ld_sem, out_sem):
        dp = lax.axis_index("dp")
        fs = lax.axis_index("fsdp")
        z, core = lax.div(fs, 2), lax.rem(fs, 2)
        gx, gy = lax.div(dp, side), lax.rem(dp, side)
        par = lax.rem(gx + gy, 2)
        up_z = (dp, lax.rem(z + 1, n_z) * 2 + core)
        dn_z = (dp, lax.rem(z + n_z - 1, n_z) * 2 + core)
        x_dev = (dp + side * (1 - 2 * lax.rem(gx, 2)), fs)
        y_dev = (dp + 1 - 2 * lax.rem(gy, 2), fs)
        sib = (dp, z * 2 + 1 - core)

        def remote(src, dst, send, recv, dev):
            return pltpu.make_async_remote_copy(src_ref=src, dst_ref=dst, send_sem=send, recv_sem=recv,
                                                device_id=dev, device_id_type=MESH)

        def spec_of(s):
            return s // per_layer, stages[s % per_layer]

        def view(s, zz, r0, nr):
            layer, (arr, c0, nc, row0, _) = spec_of(s)
            if arr == "w":
                return gw.at[layer, zz, core, pl.ds(r0, nr), pl.ds(c0, nc)]
            return gd.at[layer, zz, core, pl.ds(row0 + r0, nr), :]

        def own_pieces(s, r0, nr):
            layer, (arr, c0, nc, row0, _) = spec_of(s)
            if arr == "d":
                return [(wd_hbm.at[layer, pl.ds(row0 + r0, nr), :], view(s, z, r0, nr))]
            k = s % per_layer
            if k == 0:
                parts = [(wq_hbm, 0, n_qkv)]
            elif k == 1:
                parts = [(wo_hbm, 0, d_model), (wu_hbm, 0, n_up0)]
            else:
                parts = [(wu_hbm, n_up0, ff - n_up0)]
            out, at = [], c0
            for ref, s0, ns in parts:
                out.append((ref.at[layer, pl.ds(r0, nr), pl.ds(s0, ns)],
                            gw.at[layer, z, core, pl.ds(r0, nr), pl.ds(at, ns)]))
                at += ns
            return out

        def geometry(s):
            rows = spec_of(s)[1][4]
            half, quarter = rows // 2, rows // 4
            mine = pl.multiple_of(par * half, 16)
            other = pl.multiple_of((1 - par) * half, 16)
            return rows, half, quarter, mine, other

        def own_sends(s):
            rows, half, _, mine, _ = geometry(s)
            for src, dst in own_pieces(s, mine, half):
                remote(src, dst, z_send.at[s], z_recv.at[s, 0, 0], up_z).start()
                remote(src, dst, z_send.at[s], z_recv.at[s, 1, 0], dn_z).start()
            for src, dst in own_pieces(s, 0, rows):
                remote(src, dst, d_send.at[s], d_recv.at[s], sib).start()

        def around(d):
            return lax.rem(z - d + n_z, n_z), lax.rem(z + d, n_z)

        def z_tick(s, d):
            _, half, quarter, mine, _ = geometry(s)
            second = pl.multiple_of(mine + quarter, 16)
            lo, hi = around(d)

            @pl.when(d < far)
            def _():
                v_lo, v_hi = view(s, lo, mine, half), view(s, hi, mine, half)
                remote(v_lo, v_lo, z_send.at[s], z_recv.at[s, 0, d - 1], up_z).wait_recv()
                remote(v_hi, v_hi, z_send.at[s], z_recv.at[s, 1, d - 1], dn_z).wait_recv()

                @pl.when(d < far - 1)
                def _():
                    remote(v_lo, v_lo, z_send.at[s], z_recv.at[s, 0, d], up_z).start()
                    remote(v_hi, v_hi, z_send.at[s], z_recv.at[s, 1, d], dn_z).start()

                @pl.when(d == far - 1)
                def _():
                    q_lo, q_hi = view(s, lo, mine, quarter), view(s, hi, second, quarter)
                    remote(q_lo, q_lo, z_send.at[s], z_recv.at[s, 0, d], up_z).start()
                    remote(q_hi, q_hi, z_send.at[s], z_recv.at[s, 1, d], dn_z).start()

                for j, zz in ((0, lo), (1, hi)):
                    c_x, c_y = view(s, zz, mine, quarter), view(s, zz, second, quarter)
                    remote(c_x, c_x, c_send.at[s], x_recv.at[s, j, d - 1], x_dev).start()
                    remote(c_y, c_y, c_send.at[s], y_recv.at[s, j, d - 1], y_dev).start()

            @pl.when(d == far)
            def _():
                c_x, c_y = view(s, lo, mine, quarter), view(s, lo, second, quarter)
                remote(c_x, c_x, z_send.at[s], z_recv.at[s, 0, d - 1], up_z).wait_recv()
                remote(c_y, c_y, z_send.at[s], z_recv.at[s, 1, d - 1], dn_z).wait_recv()
                remote(c_x, c_x, c_send.at[s], x_recv.at[s, 0, d - 1], x_dev).start()
                remote(c_y, c_y, c_send.at[s], y_recv.at[s, 0, d - 1], y_dev).start()

        def d_tick(s, d):
            rows, _, quarter, _, other = geometry(s)
            second = pl.multiple_of(other + quarter, 16)
            lo, hi = around(d)

            def one(zz, j):
                c_x, c_y = view(s, zz, other, quarter), view(s, zz, second, quarter)
                remote(c_x, c_x, c_send.at[s], x_recv.at[s, j, d - 1], x_dev).wait_recv()
                remote(c_y, c_y, c_send.at[s], y_recv.at[s, j, d - 1], y_dev).wait_recv()
                whole = view(s, zz, 0, rows)
                remote(whole, whole, d_send.at[s], d_recv.at[s], sib).start()

            one(lo, 0)

            @pl.when(d < far)
            def _():
                one(hi, 1)

        def all_blocks(s, which):
            layer, (arr, c0, nc, row0, rows) = spec_of(s)
            if arr == "w":
                return gw.at[layer, :, which, :, pl.ds(c0, nc)]
            return gd.at[layer, :, which, pl.ds(row0, rows), :]

        def load_copies(s):
            layer = s // per_layer
            k = s % per_layer
            out = []
            for i in range(STEPS):
                if k == 0:
                    pairs = [(gw.at[layer, :, :, :, pl.ds(i * 3 * TILE, 3 * TILE)], w_a.at[i])]
                elif k == 1:
                    pairs = [(gw.at[layer, :, :, :, pl.ds(n_qkv + i * TILE, TILE)],
                              w_b.at[i, :, :, :, pl.ds(0, TILE)]),
                             (gw.at[layer, :, :, :, pl.ds(n_qkv + d_model + i * 2 * TILE, 2 * TILE)],
                              w_b.at[i, :, :, :, pl.ds(TILE, 2 * TILE)])]
                elif k == 2:
                    pairs = [(gw.at[layer, :, :, :, pl.ds(n_qkv + d_model + n_up0 + i * 2 * TILE, 2 * TILE)], w_c.at[i])]
                else:
                    dst = w_d0 if k == 3 else w_d1
                    pairs = [(gd.at[layer, :, :, pl.ds((k - 3) * (down_rows // 2), down_rows // 2),
                                    pl.ds(i * TILE, TILE)], dst.at[i])]
                out.append([pltpu.make_async_copy(a, b, ld_sem.at[k, i, j]) for j, (a, b) in enumerate(pairs)])
            return out

        def fetch(s):
            sibs = all_blocks(s, 1 - core)
            remote(sibs, sibs, d_send.at[s], d_recv.at[s], sib).wait_recv()
            for cps in load_copies(s):
                for cp in cps:
                    cp.start()

        def wait_load(s, i):
            k = s % per_layer
            bufs = {0: [w_a.at[i]], 1: [w_b.at[i, :, :, :, pl.ds(0, TILE)], w_b.at[i, :, :, :, pl.ds(TILE, 2 * TILE)]],
                    2: [w_c.at[i]], 3: [w_d0.at[i]], 4: [w_d1.at[i]]}[k]
            for j, buf in enumerate(bufs):
                pltpu.make_async_copy(buf, buf, ld_sem.at[k, i, j]).wait()

        x_copy = pltpu.make_async_copy(x_hbm, x_s, x_sem)
        x_copy.start()
        st = [pltpu.make_async_copy(src, dst, st_sem.at[j]) for j, (src, dst) in
              enumerate(((wq_hbm, st_q), (wo_hbm, st_o), (wu_hbm, st_u), (wd_hbm, st_d)))]
        for cp in st:
            cp.start()
        barrier = pltpu.get_barrier_semaphore()
        for dev in (up_z, dn_z, x_dev, y_dev, sib):
            pl.semaphore_signal(barrier, inc=1, device_id=dev, device_id_type=MESH)
        pl.semaphore_wait(barrier, 5)

        remote(par_ref, pg.at[z, core], p_zsend, p_zrecv.at[0, 0], up_z).start()
        remote(par_ref, pg.at[z, core], p_zsend, p_zrecv.at[1, 0], dn_z).start()
        remote(par_ref, pg.at[z, core], p_dsend, p_drecv, sib).start()
        own_sends(0)
        own_sends(1)
        pg[z, core] = par_ref[...]
        for cp in st:
            cp.wait()
        own = []
        for j, (src, c0) in enumerate(((st_q, 0), (st_o, n_qkv), (st_u, n_qkv + d_model))):
            own.append(pltpu.make_async_copy(src, gw.at[:, z, core, :, pl.ds(c0, src.shape[2])], own_sem.at[j]))
        own.append(pltpu.make_async_copy(st_d, gd.at[:, z, core], own_sem.at[3]))
        for cp in own:
            cp.start()

        def p_tick(d):
            lo, hi = around(d)
            v_lo, v_hi = pg.at[lo, core], pg.at[hi, core]
            remote(v_lo, v_lo, p_zsend, p_zrecv.at[0, d - 1], up_z).wait_recv()

            @pl.when(d < far)
            def _():
                remote(v_lo, v_lo, p_zsend, p_zrecv.at[0, d], up_z).start()
                remote(v_hi, v_hi, p_zsend, p_zrecv.at[1, d - 1], dn_z).wait_recv()

            @pl.when(d < far - 1)
            def _():
                remote(v_hi, v_hi, p_zsend, p_zrecv.at[1, d], dn_z).start()

            remote(v_lo, v_lo, p_dsend, p_drecv, sib).start()

            @pl.when(d < far)
            def _():
                remote(v_hi, v_hi, p_dsend, p_drecv, sib).start()

        @pl.loop(0, far)
        def _(i):
            p_tick(i + 1)
            z_tick(0, i + 1)

            @pl.when(i > 0)
            def _():
                d_tick(0, i)

        d_tick(0, far)

        p_all = pg.at[:, 1 - core]
        remote(p_all, p_all, p_dsend, p_drecv, sib).wait_recv()
        low = lax.broadcasted_iota(jnp.int32, (n_layers * PAR_ROWS, lanes), 1) < head_dim
        for zz in range(n_z):
            tab[:, zz * lanes:(zz + 1) * lanes] = jnp.where(low, pg[zz, 0], pg[zz, 1])
            for cc in range(2):
                at = (zz * 2 + cc) * down_rows
                for layer in range(n_layers):
                    for j in range(down_rows // lanes):
                        r = layer * PAR_ROWS + 9 + j
                        tab_up[layer:layer + 1, at + j * lanes:at + (j + 1) * lanes] = pg[zz, cc, r:r + 1, :]
        for cp in own:
            cp.wait()

        def param(layer, j, cols=None):
            r = layer * PAR_ROWS + j
            return tab[r:r + 1, :] if cols is None else tab[r:r + 1, cols]

        def norms(layer):
            @pl.loop(0, tokens // 64)
            def _(t):
                rows = pl.ds(pl.multiple_of(t * 64, 64), 64)
                xf = x_s[rows, :].astype(F32)
                mean = jnp.mean(xf, axis=-1, keepdims=True)
                cen = xf - mean
                var = jnp.mean(cen * cen, axis=-1, keepdims=True)
                nrm = cen * lax.rsqrt(var + LN_EPS)
                a_s[rows, :] = (nrm * param(layer, 0) + param(layer, 1)).astype(BF)
                m_s[rows, :] = (nrm * param(layer, 2) + param(layer, 3)).astype(BF)

        def dot(a, b):
            return jnp.dot(a, b, preferred_element_type=F32)

        def flat(ref, i):
            w = ref[i]
            return w.reshape(w.shape[0] * w.shape[1] * w.shape[2], w.shape[3])

        def rope(u):
            out = []
            for r0 in range(0, u.shape[0], seq_len):
                row = []
                for c0 in range(0, u.shape[1], lanes):
                    v = u[r0:r0 + seq_len, c0:c0 + lanes].astype(F32)
                    row.append((v * rope_ref[0] + pltpu.roll(v, lanes - half_rot, 1) * rope_ref[1]
                                + pltpu.roll(v, half_rot, 1) * rope_ref[2]).astype(BF))
                out.append(jnp.concatenate(row, axis=1))
            return jnp.concatenate(out, axis=0)

        def row_loop(block, body):
            @pl.loop(0, tokens // block)
            def _(t):
                body(pl.ds(pl.multiple_of(t * block, block), block))

        def qkv_step(layer, i):
            w = flat(w_a, i)
            cols = pl.ds(pl.multiple_of(i * TILE, TILE), TILE)

            def body(rows):
                r = dot(a_s[rows, :], w)
                q = (r[:, :TILE] + param(layer, 4, cols)).astype(BF)
                k = (r[:, TILE:2 * TILE] + param(layer, 5, cols)).astype(BF)
                q_s[rows, cols] = rope(q)
                k_s[rows, cols] = rope(k)
                v_s[rows, cols] = (r[:, 2 * TILE:] + param(layer, 6, cols)).astype(BF)

            row_loop(256, body)

        def attend(n):
            rows = pl.ds(pl.multiple_of(n * seq_len, seq_len), seq_len)
            pos_q = lax.broadcasted_iota(jnp.int32, (seq_len, seq_len), 0)
            pos_k = lax.broadcasted_iota(jnp.int32, (seq_len, seq_len), 1)
            vis = pos_k <= jnp.minimum(pos_q, lens_ref[n] - 1)
            first = lax.broadcasted_iota(jnp.int32, (seq_len, lanes), 1) < head_dim
            zero = jnp.zeros((seq_len, lanes), BF)

            for p in range(n_heads // 2):
                cs = slice(p * lanes, (p + 1) * lanes)
                q2, k2, v2 = q_s[rows, cs], k_s[rows, cs], v_s[rows, cs]
                kk = jnp.concatenate([jnp.where(first, k2, zero), jnp.where(first, zero, k2)], axis=0)
                vv = jnp.concatenate([jnp.where(first, v2, zero), jnp.where(first, zero, v2)], axis=0)
                sc = lax.dot_general(q2, kk, (((1,), (1,)), ((), ())), preferred_element_type=F32)
                probs = []
                for j in range(2):
                    s1 = jnp.where(vis, sc[:, j * seq_len:(j + 1) * seq_len] * (head_dim ** -0.5), -1e30)
                    e = jnp.exp(s1 - jnp.max(s1, axis=-1, keepdims=True))
                    probs.append((e * (1.0 / jnp.sum(e, axis=-1, keepdims=True))).astype(BF))
                ctx_s[rows, cs] = dot(jnp.concatenate(probs, axis=1), vv).astype(BF)

        def gelu_store(layer, u, rows, first_col, i, base):
            u = u + tab_up[layer:layer + 1, pl.ds(pl.multiple_of(first_col + i * 2 * TILE, 2 * TILE), 2 * TILE)]
            g = (u * 0.5 * (1.0 + lax.erf(u * (2.0 ** -0.5)))).astype(BF)
            cols = pl.ds(pl.multiple_of(base + i * TILE, TILE), TILE)
            act_a[rows, cols] = jnp.concatenate([g[:, :lanes], g[:, 2 * lanes:3 * lanes]], axis=1)
            act_b[rows, cols] = jnp.concatenate([g[:, lanes:2 * lanes], g[:, 3 * lanes:]], axis=1)

        def out_up_step(layer, i):
            w = flat(w_b, i)
            cols = pl.ds(pl.multiple_of(i * TILE, TILE), TILE)

            def body(rows):
                o = dot(ctx_s[rows, :], w[:, :TILE]) + param(layer, 7, cols)
                acc_s[rows, cols] = x_s[rows, cols].astype(F32) + o
                gelu_store(layer, dot(m_s[rows, :], w[:, TILE:]), rows, 0, i, 0)

            row_loop(256, body)

        def up_step(layer, i):
            w = flat(w_c, i)

            def body(rows):
                gelu_store(layer, dot(m_s[rows, :], w), rows, n_up0, i, n_up0 // 2)

            row_loop(256, body)

        def down0_step(layer, i):
            w = flat(w_d0, i)
            cols = pl.ds(pl.multiple_of(i * TILE, TILE), TILE)

            def body(rows):
                acc_s[rows, cols] += dot(act_a[rows, :], w)

            row_loop(256, body)

        def down1_step(layer, i):
            w = flat(w_d1, i)
            cols = pl.ds(pl.multiple_of(i * TILE, TILE), TILE)

            def body(rows):
                y = acc_s[rows, cols] + (dot(act_b[rows, :], w) + param(layer, 8, cols))
                x_s[rows, cols] = y.astype(BF)

            row_loop(256, body)

        def full_ticks(s, i):
            z_tick(s, i + 1)

            @pl.when(i > 0)
            def _():
                d_tick(s, i)

        def half_ticks(s, i, d0):
            d = d0 + lax.div(i, 2)

            @pl.when(lax.rem(i, 2) == 0)
            def _():
                z_tick(s, d)

            @pl.when(lax.rem(i, 2) == 1)
            def _():
                d_tick(s, d)

        x_copy.wait()
        norms(0)
        fetch(0)
        own_sends(2)

        for layer in range(n_layers):
            s0 = layer * per_layer
            more = layer + 1 < n_layers

            @pl.loop(0, STEPS)
            def _(i):
                half_ticks(s0 + 1, i, 1)
                wait_load(s0, i)
                qkv_step(layer, i)

            @pl.loop(0, docs // 2)
            def _(i):
                half_ticks(s0 + 1, i, 3)
                attend(i)

            own_sends(s0 + 3)

            @pl.loop(0, docs // 2)
            def _(i):
                full_ticks(s0 + 2, i)

                @pl.when(i == 2)
                def _():
                    fetch(s0 + 1)

                attend(i + docs // 2)

            d_tick(s0 + 2, far)
            own_sends(s0 + 4)

            @pl.loop(0, STEPS)
            def _(i):
                full_ticks(s0 + 3, i)

                @pl.when(i == 2)
                def _():
                    fetch(s0 + 2)

                wait_load(s0 + 1, i)
                out_up_step(layer, i)

            d_tick(s0 + 3, far)
            if more:
                own_sends(s0 + 5)

            @pl.loop(0, STEPS)
            def _(i):
                full_ticks(s0 + 4, i)

                @pl.when(i == 2)
                def _():
                    fetch(s0 + 3)

                wait_load(s0 + 2, i)
                up_step(layer, i)

            d_tick(s0 + 4, far)
            if more:
                own_sends(s0 + 6)

            @pl.loop(0, STEPS)
            def _(i):
                if more:
                    half_ticks(s0 + 5, i, 1)

                @pl.when(i == 2)
                def _():
                    fetch(s0 + 4)

                wait_load(s0 + 3, i)
                down0_step(layer, i)

            @pl.loop(0, STEPS)
            def _(i):
                if more:
                    half_ticks(s0 + 5, i, 3)
                wait_load(s0 + 4, i)
                down1_step(layer, i)
                if not more:
                    cols = pl.ds(pl.multiple_of(i * TILE, TILE), TILE)
                    pltpu.make_async_copy(x_s.at[:, cols], out_hbm.at[:, cols], out_sem.at[i]).start()

            if more:
                norms(layer + 1)
                fetch(s0 + 5)
                own_sends(s0 + 7)

        for s in range(n_layers * per_layer):
            layer, (arr, c0, nc, row0, rows) = spec_of(s)
            half = rows // 2
            if arr == "w":
                sevenths = gw.at[layer, pl.ds(0, n_z - 1), 0, pl.ds(0, half), pl.ds(c0, nc)]
            else:
                sevenths = gd.at[layer, pl.ds(0, n_z - 1), 0, pl.ds(row0, half), :]
            remote(sevenths, sevenths, z_send.at[s], z_recv.at[s, 0, 0], up_z).wait_send()
            remote(sevenths, sevenths, c_send.at[s], z_recv.at[s, 0, 0], up_z).wait_send()
            every = all_blocks(s, 0)
            remote(every, every, d_send.at[s], d_recv.at[s], sib).wait_send()
        seven = pg.at[pl.ds(0, n_z - 1), 0]
        remote(seven, seven, p_zsend, p_drecv, up_z).wait_send()
        eight = pg.at[:, 0]
        remote(eight, eight, p_dsend, p_drecv, sib).wait_send()
        for i in range(STEPS):
            cols = pl.ds(i * TILE, TILE)
            pltpu.make_async_copy(x_s.at[:, cols], out_hbm.at[:, cols], out_sem.at[i]).wait()

    n_st = n_layers * per_layer
    wide = n_qkv + d_model + ff
    out_shape = (
        jax.ShapeDtypeStruct((tokens, d_model), BF),
        jax.ShapeDtypeStruct((n_layers, n_z, 2, wide_rows, wide), BF),
        jax.ShapeDtypeStruct((n_layers, n_z, 2, down_rows, d_model), BF),
    )
    dma = pltpu.SemaphoreType.DMA
    scratch = [
        pltpu.VMEM((tokens, d_model), BF), pltpu.VMEM((tokens, d_model), BF), pltpu.VMEM((tokens, d_model), BF),
        pltpu.VMEM((tokens, d_model), BF), pltpu.VMEM((tokens, d_model), BF), pltpu.VMEM((tokens, d_model), BF),
        pltpu.VMEM((tokens, d_model), BF),
        pltpu.VMEM((tokens, ff // 2), BF), pltpu.VMEM((tokens, ff // 2), BF), pltpu.VMEM((tokens, d_model), F32),
        pltpu.VMEM((STEPS, n_z, 2, wide_rows, 3 * TILE), BF), pltpu.VMEM((STEPS, n_z, 2, wide_rows, 3 * TILE), BF),
        pltpu.VMEM((STEPS, n_z, 2, wide_rows, 2 * TILE), BF),
        pltpu.VMEM((STEPS, n_z, 2, down_rows // 2, TILE), BF), pltpu.VMEM((STEPS, n_z, 2, down_rows // 2, TILE), BF),
        pltpu.VMEM((n_layers, wide_rows, n_qkv), BF), pltpu.VMEM((n_layers, wide_rows, d_model), BF),
        pltpu.VMEM((n_layers, wide_rows, ff), BF), pltpu.VMEM((n_layers, down_rows, d_model), BF),
        pltpu.VMEM((n_z, 2, n_layers * PAR_ROWS, lanes), F32),
        pltpu.VMEM((n_layers * PAR_ROWS, d_model), F32), pltpu.VMEM((8, ff), F32),
        dma((n_st,)), dma((n_st,)), dma((n_st,)),
        dma((n_st, 2, far)), dma((n_st, 2, far)), dma((n_st, 2, far)), dma((n_st,)),
        dma(()), dma(()), dma((2, far)), dma(()),
        dma(()), dma((4,)), dma((4,)), dma((per_layer, STEPS, 2)), dma((STEPS,)),
    ]
    hbm = pl.BlockSpec(memory_space=pltpu.HBM)
    vmem = pl.BlockSpec(memory_space=pltpu.VMEM)
    smem = pl.BlockSpec(memory_space=pltpu.SMEM)
    return pl.pallas_call(
        kernel,
        name="layers",
        out_shape=out_shape,
        in_specs=[hbm, smem, vmem, vmem, hbm, hbm, hbm, hbm],
        out_specs=(hbm, hbm, hbm),
        scratch_shapes=scratch,
        compiler_params=pltpu.CompilerParams(collective_id=0, has_side_effects=True, vmem_limit_bytes=67043328),
    )


def solution(mesh):
    row_spec = P(('dp', 'fsdp'), None, None)
    in_specs = (row_spec, P(('dp', 'fsdp')), P(None, None, 'fsdp'), P(None, 'fsdp', None, None), P(None, 'fsdp'), P(None, 'fsdp', None), P(None, 'fsdp'), P(None, 'fsdp', None), P(None, 'fsdp'), P(None, 'fsdp', None), P(None, 'fsdp'))
    n_z = mesh.shape['fsdp'] // 2
    side = math.isqrt(mesh.shape['dp'])

    def local_step(hidden, lens, ln_par, w_qkv, b_qkv, w_out, b_out, w_up, b_up, w_down, b_down):
        docs, seq_len, d_model = hidden.shape
        n_layers, rows, n_heads, triple = w_qkv.shape
        head_dim = triple // 3
        ff = w_up.shape[2]
        per_tile = TILE // head_dim
        wq = w_qkv.reshape(n_layers, rows, n_heads // per_tile, per_tile, 3, head_dim)
        wq = wq.transpose(0, 1, 2, 4, 3, 5).reshape(n_layers, rows, 3 * d_model)
        small = jnp.concatenate([ln_par, b_qkv.astype(F32).reshape(n_layers, 3, -1), b_out.astype(F32)[:, None],
                                 b_down.astype(F32)[:, None]], axis=1)
        small = jnp.concatenate([small, small], axis=2)
        small = jnp.concatenate([small, b_up.astype(F32).reshape(n_layers, -1, 2 * head_dim)], axis=1)
        small = jnp.pad(small, ((0, 0), (0, PAR_ROWS - small.shape[1]), (0, 0))).reshape(-1, 2 * head_dim)
        rope = jnp.asarray(rotary_lanes(seq_len, head_dim))
        call = make_kernel(n_layers, n_z, side, docs, seq_len, d_model, n_heads, ff)
        out = call(hidden.reshape(docs * seq_len, d_model), lens, small, rope, wq, w_out, w_up, w_down)[0]
        return out.reshape(docs, seq_len, d_model)

    return jax.shard_map(local_step, mesh=mesh, in_specs=in_specs, out_specs=row_spec, check_vma=False)
```

time: 540 us -> 273 us (0.51); the launches traced: 529 us -> 272 us
  Pallas kernels: 0 us -> 259 us
  matrix products: 175 us -> 0 us
  local copies, waits for them, and re-layouts: 180 us -> 10.6 us
  blocking collectives: 124 us -> 0 us
  other arithmetic: 30.5 us -> 2.76 us
  between operations: 15.9 us -> 0.03 us
    pallas_call x0 -> x1, Pallas kernels: none -> 259 us  [local_step(): call(hidden.reshape(docs * seq_len, d_model), lens, small, rope, wq, w_ou...]
    dot_general x12 -> x0, matrix products: 175 us -> none  [the longest x2 97.5 us: layer_forward(): jnp.dot(mlp_in, w_up_full, preferred_element_type=jnp.float32)]
    slice x20 -> x0, local copies, waits for them, and re-layouts: 75.6 us -> none  [the longest x2 43.8 us: layer_forward(): mlp_in = layer_norm(x_rows, ln_full[2], ln_full[3])]
    all_gather x4 -> x0, blocking collectives: 71.1 us -> none  [gather_full(): return lax.all_gather(piece, 'fsdp', axis=axis_idx, tiled=True)]
    unnamed x1 -> x0, blocking collectives: 53.1 us -> none
    unnamed x88 -> x2, local copies, waits for them, and re-layouts: 47.5 us -> 5.39 us
    reshape x2 -> x3, local copies, waits for them, and re-layouts: 29.3 us -> 3.33 us  [the longest x1 1.88 us: local_step(): wq = wq.transpose(0, 1, 2, 4, 3, 5).reshape(n_layers, rows, 3 * d_model)]
    all_gather x2 -> x0, local copies, waits for them, and re-layouts: 24 us -> none  [gather_full(): return lax.all_gather(piece, 'fsdp', axis=axis_idx, tiled=True)]
  transfers between devices with their start and end apart: 8 -> 0, of which waited for: 0 -> 0; matrix products, arithmetic and copies ran while one was open for 69% -> 0% of each run, Pallas kernels for 0% -> 0%
where the time goes in v1:
time: 273 us; the launch traced here: 272 us
  Pallas kernels  259 us (95%)
  local copies, waits for them, and re-layouts  10.6 us (4%)
  other arithmetic  2.76 us (1%)
    pallas_call x1, Pallas kernels, local_step(): call(hidden.reshape(docs * seq_len, d_model), lens, small, rope, wq, w_ou...  259 us

profile of v1, /device:TPU:21, one launch (start us, length us, event | category | flops | bytes accessed | tf_op | source)
XLA Modules:
  0.0 272.1 jit_solution(7780627651519150620)
XLA Ops:
  0.0 0.7 bitcast_convert_fusion.1
  0.7 0.7 bitcast_convert_fusion
  1.3 0.7 reshape.41
  2.0 0.8 reshape.37
  2.8 1.4 select_maximum_fusion
  4.2 2.3 copy.18
  6.5 1.9 copy.19
  8.4 1.9 reshape.34.wq_hbm
  10.3 258.7 %layers.1 = (bf16[1024,1024]{1,0:T(8,128)(2,1)}, bf16[2,8,2,64,8192]{4,3,2,1,0:T(8,128)(2,1)}, bf16[2,8,2,256,1024]{4,3,2,1,0:T(8,128)(2,1)}) custom-call(bf16[1024,1024]{1,0:T(8,128)(2,1)} %bitcast.15, s32[8]{0:T(128)} %lens_ref.1, f32[32,128]{1,0:T(8,128)} %bitcast.17, f32[3,128,128]{2,1,0:T(8,128)} %constant.5.clone.rope_ref, ...), custom_call_target="tpu_custom_call" | custom-call | tf_op jit(solution)/shard_map/layers/pallas_call | solution.py:598
  269.0 3.1 %copy.21 = bf16[8,128,1024]{2,1,0:T(8,128)(2,1)} copy(bf16[8,128,1024]{2,1,0:T(8,128)(2,1)} %bitcast.16) | data formatting | bytes 4194304

commit v2 on v0

v2 whole, which is shorter than its diff:
```python
import math

import jax
import jax.numpy as jnp
import numpy as np
from jax import lax
from jax.experimental import pallas as pl
from jax.experimental.pallas import tpu as pltpu
from jax.sharding import PartitionSpec as P

MESH = pl.DeviceIdType.MESH
ROPE_BASE = 10000.0
LN_EPS = 1e-5
BF = jnp.bfloat16
F32 = jnp.float32
TILE = 256
BLOCKS = 4
PAR_ROWS = 16


def rotary_lanes(seq_len, head_dim):
    rot = head_dim // 4
    half = rot // 2
    inv_freq = (1.0 / (ROPE_BASE ** (np.arange(0, rot, 2, dtype=np.float32) / rot))).astype(np.float32)
    angles = np.arange(seq_len, dtype=np.float32)[:, None] * inv_freq[None, :]
    cos_v, sin_v = np.cos(angles), np.sin(angles)
    tab = np.zeros((3, seq_len, 2 * head_dim), np.float32)
    tab[0] = 1.0
    for base in (0, head_dim):
        tab[0, :, base:base + half] = cos_v
        tab[0, :, base + half:base + rot] = cos_v
        tab[1, :, base:base + half] = -sin_v
        tab[2, :, base + half:base + rot] = sin_v
    return tab


def make_kernel(n_layers, n_z, side, docs, seq_len, d_model, n_heads, ff):
    head_dim = d_model // n_heads
    half_rot = head_dim // 8
    tokens = docs * seq_len
    lanes = 2 * head_dim
    rows_w = d_model // (2 * n_z)
    down_rows = ff // (2 * n_z)
    n_up = ff // d_model
    far = n_z // 2
    half, quarter = rows_w // 2, rows_w // 4
    per_layer = 4 + 2 * n_up
    n_st = n_layers * per_layer
    d_cols = d_model // n_up
    parts = down_rows // rows_w
    blk = tokens // BLOCKS

    def kernel(x_hbm, lens_ref, par_ref, rope_ref, wq_hbm, wo_hbm, wu_hbm, wd_hbm,
               out_hbm, g,
               x_s, a_s, m_s, qkv_s, ctx_s, act_s, acc_s, w_s, wd_s, st_q, st_o, st_u, st_d,
               pg, tab, tab_up,
               z_send, c_send, d_send, z_recv, x_recv, y_recv, d_recv,
               p_zsend, p_dsend, p_zrecv, p_drecv,
               x_sem, st_sem, own_sem, ld_sem, ldd_sem, out_sem):
        dp = lax.axis_index("dp")
        fs = lax.axis_index("fsdp")
        z, core = lax.div(fs, 2), lax.rem(fs, 2)
        gx, gy = lax.div(dp, side), lax.rem(dp, side)
        par = lax.rem(gx + gy, 2)
        up_z = (dp, lax.rem(z + 1, n_z) * 2 + core)
        dn_z = (dp, lax.rem(z + n_z - 1, n_z) * 2 + core)
        x_dev = (dp + side * (1 - 2 * lax.rem(gx, 2)), fs)
        y_dev = (dp + 1 - 2 * lax.rem(gy, 2), fs)
        sib = (dp, z * 2 + 1 - core)
        mine = pl.multiple_of(par * half, 16)
        mine2 = pl.multiple_of(par * half + quarter, 16)
        other = pl.multiple_of((1 - par) * half, 16)
        other2 = pl.multiple_of((1 - par) * half + quarter, 16)

        def remote(src, dst, send, recv, dev):
            return pltpu.make_async_remote_copy(src_ref=src, dst_ref=dst, send_sem=send, recv_sem=recv,
                                                device_id=dev, device_id_type=MESH)

        def same(ref, send, recv, dev):
            return remote(ref, ref, send, recv, dev)

        def view(s, zz, r0, nr):
            return g.at[s, zz, core, pl.ds(r0, nr), :]

        def around(d):
            return lax.rem(z - d + n_z, n_z), lax.rem(z + d, n_z)

        def guard(s, fn):
            if isinstance(s, int):
                if 0 <= s < n_st:
                    fn()
            else:
                pl.when(s < n_st)(fn)

        def own_send(s, src=None):
            piece = view(s, z, mine, half) if src is None else src(mine, half)
            whole = view(s, z, 0, rows_w) if src is None else src(0, rows_w)
            remote(piece, view(s, z, mine, half), z_send.at[s], z_recv.at[s, 0, 0], up_z).start()
            remote(piece, view(s, z, mine, half), z_send.at[s], z_recv.at[s, 1, 0], dn_z).start()
            remote(whole, view(s, z, 0, rows_w), d_send.at[s], d_recv.at[s], sib).start()

        def z_hop(s, d):
            lo, hi = around(d)
            if d == far:
                c_x, c_y = view(s, lo, mine, quarter), view(s, lo, mine2, quarter)
                same(c_x, z_send.at[s], z_recv.at[s, 0, d - 1], up_z).wait_recv()
                same(c_x, c_send.at[s], x_recv.at[s, 0, d - 1], x_dev).start()
                same(c_y, z_send.at[s], z_recv.at[s, 1, d - 1], dn_z).wait_recv()
                same(c_y, c_send.at[s], y_recv.at[s, 0, d - 1], y_dev).start()
                return
            for j, zz, nxt in ((0, lo, up_z), (1, hi, dn_z)):
                v = view(s, zz, mine, half)
                same(v, z_send.at[s], z_recv.at[s, j, d - 1], nxt).wait_recv()
                if d == far - 1:
                    v = view(s, zz, (mine, mine2)[j], quarter)
                same(v, z_send.at[s], z_recv.at[s, j, d], nxt).start()
                c_x, c_y = view(s, zz, mine, quarter), view(s, zz, mine2, quarter)
                same(c_x, c_send.at[s], x_recv.at[s, j, d - 1], x_dev).start()
                same(c_y, c_send.at[s], y_recv.at[s, j, d - 1], y_dev).start()

        def d_hop(s, d):
            for j, zz in enumerate(around(d)[:1 if d == far else 2]):
                c_x, c_y = view(s, zz, other, quarter), view(s, zz, other2, quarter)
                same(c_x, c_send.at[s], x_recv.at[s, j, d - 1], x_dev).wait_recv()
                same(c_y, c_send.at[s], y_recv.at[s, j, d - 1], y_dev).wait_recv()
                same(view(s, zz, 0, rows_w), d_send.at[s], d_recv.at[s], sib).start()

        def tick_z(t):
            for d in range(far, 0, -1):
                guard(t - d + 1, lambda d=d: z_hop(t - d + 1, d))
            guard(t + 2, lambda: own_send(t + 2))

        def tick_d(t):
            for d in range(far, 0, -1):
                guard(t - d, lambda d=d: d_hop(t - d, d))

        def loads(s, slot, down):
            if not down:
                return [pltpu.make_async_copy(g.at[s], w_s.at[slot], ld_sem.at[slot])]
            return [pltpu.make_async_copy(g.at[s, :, :, :, pl.ds(q * d_cols, d_cols)],
                                          wd_s.at[slot, :, :, pl.ds(q * rows_w, rows_w), :], ldd_sem.at[slot, q])
                    for q in range(parts)]

        def fetch(s, slot, down=False):
            sibs = g.at[s, :, 1 - core]
            same(sibs, d_send.at[s], d_recv.at[s], sib).wait_recv()
            for cp in loads(s, slot, down):
                cp.start()

        x_copy = pltpu.make_async_copy(x_hbm, x_s, x_sem)
        st = [pltpu.make_async_copy(src, dst, st_sem.at[j]) for j, (src, dst) in
              enumerate(((wq_hbm, st_q), (wo_hbm, st_o), (wu_hbm, st_u), (wd_hbm, st_d)))]
        for cp in st:
            cp.start()
        x_copy.start()
        barrier = pltpu.get_barrier_semaphore()
        for dev in (up_z, dn_z, x_dev, y_dev, sib):
            pl.semaphore_signal(barrier, inc=1, device_id=dev, device_id_type=MESH)
        pl.semaphore_wait(barrier, 5)

        remote(par_ref, pg.at[z, core], p_zsend, p_zrecv.at[0, 0], up_z).start()
        remote(par_ref, pg.at[z, core], p_zsend, p_zrecv.at[1, 0], dn_z).start()
        remote(par_ref, pg.at[z, core], p_dsend, p_drecv, sib).start()
        for s in range(2):
            own_send(s, lambda r0, nr, s=s: wq_hbm.at[0, pl.ds(r0, nr), pl.ds(s * d_model, d_model)])
        pg[z, core] = par_ref[...]
        for cp in st:
            cp.wait()
        own = []
        for layer in range(n_layers):
            pieces = [(0, st_q.at[layer, :, pl.ds(j * d_model, d_model)], j) for j in range(3)]
            pieces.append((0, st_o.at[layer], 3))
            pieces += [(0, st_u.at[layer, :, pl.ds(j * d_model, d_model)], 4 + j) for j in range(n_up)]
            for j in range(n_up):
                for q in range(parts):
                    pieces.append((q, st_d.at[layer, pl.ds(q * rows_w, rows_w), pl.ds(j * d_cols, d_cols)], 4 + n_up + j))
            for q, src, j in pieces:
                dst = g.at[layer * per_layer + j, z, core]
                if j >= 4 + n_up:
                    dst = g.at[layer * per_layer + j, z, core, :, pl.ds(q * d_cols, d_cols)]
                own.append(pltpu.make_async_copy(src, dst, own_sem.at[len(own)]))
        for cp in own:
            cp.start()
        for cp in own:
            cp.wait()

        def p_hop(d):
            lo, hi = around(d)
            v_lo, v_hi = pg.at[lo, core], pg.at[hi, core]
            same(v_lo, p_zsend, p_zrecv.at[0, d - 1], up_z).wait_recv()
            if d < far:
                same(v_lo, p_zsend, p_zrecv.at[0, d], up_z).start()
                same(v_hi, p_zsend, p_zrecv.at[1, d - 1], dn_z).wait_recv()
            if d < far - 1:
                same(v_hi, p_zsend, p_zrecv.at[1, d], dn_z).start()
            same(v_lo, p_dsend, p_drecv, sib).start()
            if d < far:
                same(v_hi, p_dsend, p_drecv, sib).start()

        for t in range(far):
            p_hop(t + 1)
            tick_z(t)
            tick_d(t)
        tick_z(far)
        tick_d(far)

        p_all = pg.at[:, 1 - core]
        same(p_all, p_dsend, p_drecv, sib).wait_recv()
        low = lax.broadcasted_iota(jnp.int32, (PAR_ROWS, lanes), 1) < head_dim
        for layer in range(n_layers):
            r0 = layer * PAR_ROWS
            for zz in range(n_z):
                tab[layer, :, zz * lanes:(zz + 1) * lanes] = jnp.where(
                    low, pg[zz, 0, r0:r0 + PAR_ROWS, :], pg[zz, 1, r0:r0 + PAR_ROWS, :])
                for cc in range(2):
                    at = (zz * 2 + cc) * down_rows
                    for j in range(down_rows // lanes):
                        r = r0 + 9 + j
                        tab_up[layer, 0:1, at + j * lanes:at + (j + 1) * lanes] = pg[zz, cc, r:r + 1, :]
            for b in range(3 * n_z):
                two = []
                for p in (2 * b, 2 * b + 1):
                    dev, r = p // 3, r0 + 4 + p % 3
                    two.append(pg[dev // 2, dev % 2, r:r + 1, :])
                c0 = (b % n_z) * lanes
                tab[layer, 4 + b // n_z:5 + b // n_z, c0:c0 + lanes] = jnp.where(low[0:1], two[0], two[1])

        def norms(layer):
            @pl.loop(0, tokens // 64)
            def _(t):
                rows = pl.ds(pl.multiple_of(t * 64, 64), 64)
                xf = x_s[rows, :].astype(F32)
                mean = jnp.mean(xf, axis=-1, keepdims=True)
                cen = xf - mean
                var = jnp.mean(cen * cen, axis=-1, keepdims=True)
                nrm = cen * lax.rsqrt(var + LN_EPS)
                a_s[rows, :] = (nrm * tab[layer, 0:1, :] + tab[layer, 1:2, :]).astype(BF)
                m_s[rows, :] = (nrm * tab[layer, 2:3, :] + tab[layer, 3:4, :]).astype(BF)

        def dot(a, b):
            return jnp.dot(a, b, preferred_element_type=F32)

        def rows_of(r):
            return pl.ds(pl.multiple_of(r * blk, blk), blk)

        def w_tile(slot, c0, nc):
            return w_s[slot, :, :, :, c0:c0 + nc].reshape(d_model, nc)

        def qkv_block(layer, j, slot, r):
            rows = rows_of(r)
            for c0 in range(0, d_model, TILE):
                y = dot(a_s[rows, :], w_tile(slot, c0, TILE)) + tab[layer, pl.ds(4 + j, 1), c0:c0 + TILE]
                qkv_s[j, rows, c0:c0 + TILE] = y.astype(BF)

        def attend(n):
            rows = pl.ds(pl.multiple_of(n * seq_len, seq_len), seq_len)
            pos_q = lax.broadcasted_iota(jnp.int32, (seq_len, seq_len), 0)
            pos_k = lax.broadcasted_iota(jnp.int32, (seq_len, seq_len), 1)
            vis = pos_k <= jnp.minimum(pos_q, lens_ref[n] - 1)
            first = lax.broadcasted_iota(jnp.int32, (seq_len, lanes), 1) < head_dim
            zero = jnp.zeros((seq_len, lanes), BF)

            def rope(v):
                v = v.astype(F32)
                return (v * rope_ref[0] + pltpu.roll(v, lanes - half_rot, 1) * rope_ref[1]
                        + pltpu.roll(v, half_rot, 1) * rope_ref[2]).astype(BF)

            for p in range(n_heads // 2):
                cs = slice(p * lanes, (p + 1) * lanes)
                trio = []
                for b in range(3 * p, 3 * p + 3):
                    trio.append(qkv_s[b // n_z, rows, (b % n_z) * lanes:(b % n_z + 1) * lanes])
                q2 = rope(jnp.where(first, trio[0], trio[1]))
                k2 = rope(pltpu.roll(jnp.where(first, trio[2], trio[0]).astype(F32), head_dim, 1))
                v2 = jnp.where(first, trio[1], trio[2])
                kk = jnp.concatenate([jnp.where(first, k2, zero), jnp.where(first, zero, k2)], axis=0)
                vv = jnp.concatenate([jnp.where(first, v2, zero), jnp.where(first, zero, v2)], axis=0)
                sc = lax.dot_general(q2, kk, (((1,), (1,)), ((), ())), preferred_element_type=F32)
                probs = []
                for j in range(2):
                    s1 = jnp.where(vis, sc[:, j * seq_len:(j + 1) * seq_len] * (head_dim ** -0.5), -1e30)
                    e = jnp.exp(s1 - jnp.max(s1, axis=-1, keepdims=True))
                    probs.append((e * (1.0 / jnp.sum(e, axis=-1, keepdims=True))).astype(BF))
                ctx_s[rows, cs] = dot(jnp.concatenate(probs, axis=1), vv).astype(BF)

        def out_block(layer, slot, r):
            rows = rows_of(r)
            for c0 in range(0, d_model, TILE):
                cols = slice(c0, c0 + TILE)
                o = dot(ctx_s[rows, :], w_tile(slot, c0, TILE)) + tab[layer, 7:8, cols]
                acc_s[rows, cols] = x_s[rows, cols].astype(F32) + o

        def up_block(layer, j, slot, r):
            rows = rows_of(r)
            for c0 in range(0, d_model, TILE):
                cols = pl.ds(pl.multiple_of(j * d_model + c0, TILE), TILE)
                u = dot(m_s[rows, :], w_tile(slot, c0, TILE)) + tab_up[layer, 0:1, cols]
                act_s[rows, cols] = (u * 0.5 * (1.0 + lax.erf(u * (2.0 ** -0.5)))).astype(BF)

        def down_block(layer, j, slot, r):
            rows = rows_of(r)
            cols = pl.ds(pl.multiple_of(j * d_cols, d_cols), d_cols)
            w = wd_s[slot].reshape(ff, d_cols)
            y = acc_s[rows, cols] + (dot(act_s[rows, :], w) + tab[layer, 8:9, cols])
            x_s[rows, cols] = y.astype(BF)

        def out_copy(j):
            cols = pl.ds(pl.multiple_of(j * d_cols, d_cols), d_cols)
            return pltpu.make_async_copy(x_s.at[:, cols], out_hbm.at[:, cols], out_sem.at[j])

        x_copy.wait()
        norms(0)
        fetch(0, 0)

        @pl.loop(0, n_layers)
        def _(layer):
            s0 = layer * per_layer
            t0 = s0 + far + 1

            @pl.loop(0, 3)
            def _(j):
                slot = lax.rem(j, 2)

                @pl.loop(0, BLOCKS)
                def _(r):
                    @pl.when(r == 0)
                    def _():
                        tick_z(t0 + j)
                        loads(s0 + j, slot, False)[0].wait()

                    @pl.when(r == 2)
                    def _():
                        tick_d(t0 + j)

                    qkv_block(layer, j, slot, r)

                    @pl.when(r == BLOCKS - 1)
                    def _():
                        fetch(s0 + j + 1, 1 - slot)

            @pl.loop(0, docs)
            def _(n):
                t = t0 + 3 + lax.div(n, docs // 2)

                @pl.when(lax.rem(n, docs // 2) == 0)
                def _():
                    tick_z(t)

                @pl.when(lax.rem(n, docs // 2) == 2)
                def _():
                    tick_d(t)

                attend(n)

            loads(s0 + 3, 1, False)[0].wait()
            fetch(s0 + 4, 0)

            @pl.loop(0, BLOCKS)
            def _(r):
                out_block(layer, 1, r)

            @pl.loop(0, n_up)
            def _(j):
                slot = lax.rem(j, 2)

                @pl.loop(0, BLOCKS)
                def _(r):
                    @pl.when(r == 0)
                    def _():
                        tick_z(t0 + 5 + j)
                        loads(s0 + 4 + j, slot, False)[0].wait()

                    @pl.when(r == 2)
                    def _():
                        tick_d(t0 + 5 + j)

                    up_block(layer, j, slot, r)

                    @pl.when((r == BLOCKS - 1) & (j < n_up - 1))
                    def _():
                        fetch(s0 + 5 + j, 1 - slot)

                    @pl.when((r == BLOCKS - 1) & (j == n_up - 1))
                    def _():
                        fetch(s0 + 4 + n_up, 0, True)

            @pl.loop(0, n_up)
            def _(j):
                slot = lax.rem(j, 2)

                @pl.loop(0, BLOCKS)
                def _(r):
                    @pl.when((r == 0) & (j < n_up - 1))
                    def _():
                        tick_z(t0 + 5 + n_up + j)

                    @pl.when(r == 0)
                    def _():
                        for cp in loads(s0 + 4 + n_up + j, slot, True):
                            cp.wait()

                    @pl.when((r == 2) & (j < n_up - 1))
                    def _():
                        tick_d(t0 + 5 + n_up + j)

                    down_block(layer, j, slot, r)

                    @pl.when((r == BLOCKS - 1) & (j < n_up - 1))
                    def _():
                        fetch(s0 + 5 + n_up + j, 1 - slot, True)

                    @pl.when((r == BLOCKS - 1) & (j == n_up - 1) & (layer < n_layers - 1))
                    def _():
                        fetch(s0 + per_layer, 0)

                @pl.when(layer == n_layers - 1)
                def _():
                    out_copy(j).start()

            @pl.when(layer < n_layers - 1)
            def _():
                norms(layer + 1)

        @pl.loop(0, n_st)
        def _(s):
            sevenths = g.at[s, pl.ds(0, n_z - 1), 0, pl.ds(0, half), :]
            same(sevenths, z_send.at[s], z_recv.at[s, 0, 0], up_z).wait_send()
            same(sevenths, c_send.at[s], z_recv.at[s, 0, 0], up_z).wait_send()
            same(g.at[s, :, 0], d_send.at[s], d_recv.at[s], sib).wait_send()

        seven = pg.at[pl.ds(0, n_z - 1), 0]
        same(seven, p_zsend, p_drecv, up_z).wait_send()
        eight = pg.at[:, 0]
        same(eight, p_dsend, p_drecv, sib).wait_send()
        for j in range(n_up):
            out_copy(j).wait()

    out_shape = (
        jax.ShapeDtypeStruct((tokens, d_model), BF),
        jax.ShapeDtypeStruct((n_st, n_z, 2, rows_w, d_model), BF),
    )
    dma = pltpu.SemaphoreType.DMA
    n_own = n_layers * (4 + n_up + n_up * parts)
    act = pltpu.VMEM((tokens, d_model), BF)
    scratch = [
        act, act, act, pltpu.VMEM((3, tokens, d_model), BF), act, pltpu.VMEM((tokens, ff), BF),
        pltpu.VMEM((tokens, d_model), F32),
        pltpu.VMEM((2, n_z, 2, rows_w, d_model), BF), pltpu.VMEM((2, n_z, 2, down_rows, d_cols), BF),
        pltpu.VMEM((n_layers, rows_w, 3 * d_model), BF), pltpu.VMEM((n_layers, rows_w, d_model), BF),
        pltpu.VMEM((n_layers, rows_w, ff), BF), pltpu.VMEM((n_layers, down_rows, d_model), BF),
        pltpu.VMEM((n_z, 2, n_layers * PAR_ROWS, lanes), F32),
        pltpu.VMEM((n_layers, PAR_ROWS, d_model), F32), pltpu.VMEM((n_layers, 8, ff), F32),
        dma((n_st,)), dma((n_st,)), dma((n_st,)),
        dma((n_st, 2, far)), dma((n_st, 2, far)), dma((n_st, 2, far)), dma((n_st,)),
        dma(()), dma(()), dma((2, far)), dma(()),
        dma(()), dma((4,)), dma((n_own,)), dma((2,)), dma((2, parts)), dma((n_up,)),
    ]
    hbm = pl.BlockSpec(memory_space=pltpu.HBM)
    vmem = pl.BlockSpec(memory_space=pltpu.VMEM)
    smem = pl.BlockSpec(memory_space=pltpu.SMEM)
    return pl.pallas_call(
        kernel,
        name="layers",
        out_shape=out_shape,
        in_specs=[hbm, smem, vmem, vmem, hbm, hbm, hbm, hbm],
        out_specs=(hbm, hbm),
        scratch_shapes=scratch,
        compiler_params=pltpu.CompilerParams(collective_id=0, has_side_effects=True, vmem_limit_bytes=67043328),
    )


def solution(mesh):
    row_spec = P(('dp', 'fsdp'), None, None)
    in_specs = (row_spec, P(('dp', 'fsdp')), P(None, None, 'fsdp'), P(None, 'fsdp', None, None), P(None, 'fsdp'), P(None, 'fsdp', None), P(None, 'fsdp'), P(None, 'fsdp', None), P(None, 'fsdp'), P(None, 'fsdp', None), P(None, 'fsdp'))
    n_z = mesh.shape['fsdp'] // 2
    side = math.isqrt(mesh.shape['dp'])

    def local_step(hidden, lens, ln_par, w_qkv, b_qkv, w_out, b_out, w_up, b_up, w_down, b_down):
        docs, seq_len, d_model = hidden.shape
        n_layers, rows, n_heads, triple = w_qkv.shape
        head_dim = triple // 3
        ff = w_up.shape[2]
        wq = w_qkv.reshape(n_layers, rows, n_heads * triple)
        small = jnp.concatenate([ln_par, b_qkv.astype(F32).reshape(n_layers, 3, -1), b_out.astype(F32)[:, None],
                                 b_down.astype(F32)[:, None]], axis=1)
        small = jnp.concatenate([small, small], axis=2)
        small = jnp.concatenate([small, b_up.astype(F32).reshape(n_layers, -1, 2 * head_dim)], axis=1)
        small = jnp.pad(small, ((0, 0), (0, PAR_ROWS - small.shape[1]), (0, 0))).reshape(-1, 2 * head_dim)
        rope = jnp.asarray(rotary_lanes(seq_len, head_dim))
        call = make_kernel(n_layers, n_z, side, docs, seq_len, d_model, n_heads, ff)
        out = call(hidden.reshape(docs * seq_len, d_model), lens, small, rope, wq, w_out, w_up, w_down)[0]
        return out.reshape(docs, seq_len, d_model)

    return jax.shard_map(local_step, mesh=mesh, in_specs=in_specs, out_specs=row_spec, check_vma=False)
```

time: 540 us -> 203 us (0.38); the launches traced: 529 us -> 201 us
  Pallas kernels: 0 us -> 191 us
  matrix products: 175 us -> 0 us
  local copies, waits for them, and re-layouts: 180 us -> 7.39 us
  blocking collectives: 124 us -> 0 us
  other arithmetic: 30.5 us -> 2.76 us
  between operations: 15.9 us -> 0.01 us
    pallas_call x0 -> x1, Pallas kernels: none -> 191 us  [local_step(): call(hidden.reshape(docs * seq_len, d_model), lens, small, rope, wq, w_ou...]
    dot_general x12 -> x0, matrix products: 175 us -> none  [the longest x2 97.5 us: layer_forward(): jnp.dot(mlp_in, w_up_full, preferred_element_type=jnp.float32)]
    slice x20 -> x0, local copies, waits for them, and re-layouts: 75.6 us -> none  [the longest x2 43.8 us: layer_forward(): mlp_in = layer_norm(x_rows, ln_full[2], ln_full[3])]
    all_gather x4 -> x0, blocking collectives: 71.1 us -> none  [gather_full(): return lax.all_gather(piece, 'fsdp', axis=axis_idx, tiled=True)]
    unnamed x1 -> x0, blocking collectives: 53.1 us -> none
    unnamed x88 -> x1, local copies, waits for them, and re-layouts: 47.5 us -> 3.08 us
    reshape x2 -> x3, local copies, waits for them, and re-layouts: 29.3 us -> 4.31 us  [the longest x1 2.86 us: local_step(): wq = w_qkv.reshape(n_layers, rows, n_heads * triple)]
    all_gather x2 -> x0, local copies, waits for them, and re-layouts: 24 us -> none  [gather_full(): return lax.all_gather(piece, 'fsdp', axis=axis_idx, tiled=True)]
  transfers between devices with their start and end apart: 8 -> 0, of which waited for: 0 -> 0; matrix products, arithmetic and copies ran while one was open for 69% -> 0% of each run, Pallas kernels for 0% -> 0%
where the time goes in v2:
time: 203 us; the launch traced here: 201 us
  Pallas kernels  191 us (94%)
  local copies, waits for them, and re-layouts  7.39 us (4%)
  other arithmetic  2.76 us (1%)
    pallas_call x1, Pallas kernels, local_step(): call(hidden.reshape(docs * seq_len, d_model), lens, small, rope, wq, w_ou...  191 us

profile of v2, /device:TPU:21, one launch (start us, length us, event | category | flops | bytes accessed | tf_op | source)
XLA Modules:
  0.0 201.3 jit_solution(16197987824420657623)
XLA Ops:
  0.0 0.7 bitcast_convert_fusion.1
  0.7 0.7 bitcast_convert_fusion
  1.3 0.7 reshape.37
  2.0 0.8 reshape.33
  2.8 1.4 select_maximum_fusion
  4.2 2.9 %reshape.30.wq_hbm = bf16[2,64,3072]{2,1,0:T(8,128)(2,1)} reshape(bf16[2,64,16,192]{3,2,1,0:T(8,128)(2,1)} %param.15) | data formatting | bytes 1572864 | tf_op jit(solution)/shard_map/reshape | solution.py:483
  7.1 191.2 %layers.1 = (bf16[1024,1024]{1,0:T(8,128)(2,1)}, bf16[24,8,2,64,1024]{4,3,2,1,0:T(8,128)(2,1)}) custom-call(bf16[1024,1024]{1,0:T(8,128)(2,1)} %bitcast.13, s32[8]{0:T(128)} %lens_ref.1, f32[32,128]{1,0:T(8,128)} %bitcast.15, f32[3,128,128]{2,1,0:T(8,128)} %constant.5.clone.rope_ref, bf16[2,64,3072]{2,1,0:T(8,128)(2,1)} %reshape.30.wq_hbm, ...), custom_call_target="tpu_custom_call" | custom-call | tf_op jit(solution)/shard_map/layers/pallas_call | solution.py:491
  198.2 3.1 %copy.18 = bf16[8,128,1024]{2,1,0:T(8,128)(2,1)} copy(bf16[8,128,1024]{2,1,0:T(8,128)(2,1)} %bitcast.14) | data formatting | bytes 4194304

commit v3 on v2

--- a/solution.py
+++ b/solution.py
@@ -49,6 +49,8 @@
     d_cols = d_model // n_up
     parts = down_rows // rows_w
     blk = tokens // BLOCKS
+    n_slots = 4 * per_layer
+    n_blocks = BLOCKS * (5 + 2 * n_up) + docs
 
     def kernel(x_hbm, lens_ref, par_ref, rope_ref, wq_hbm, wo_hbm, wu_hbm, wd_hbm,
                out_hbm, g,
@@ -125,14 +127,22 @@
                 same(c_y, c_send.at[s], y_recv.at[s, j, d - 1], y_dev).wait_recv()
                 same(view(s, zz, 0, rows_w), d_send.at[s], d_recv.at[s], sib).start()
 
-        def tick_z(t):
-            for d in range(far, 0, -1):
-                guard(t - d + 1, lambda d=d: z_hop(t - d + 1, d))
-            guard(t + 2, lambda: own_send(t + 2))
-
-        def tick_d(t):
-            for d in range(far, 0, -1):
-                guard(t - d, lambda d=d: d_hop(t - d, d))
+        def slot(t, k):
+            for s, d in (((t, 1),), ((t - 1, 2),), ((t - 3, 4), (t - 2, 3)), ())[k]:
+                guard(s, lambda s=s, d=d: z_hop(s, d))
+            for s, d in (((t - 1, 1),), ((t - 2, 2),), ((t - 4, 4), (t - 3, 3)), ())[k]:
+                guard(s, lambda s=s, d=d: d_hop(s, d))
+            if k == 3:
+                guard(t + 2, lambda: own_send(t + 2))
+
+        def slots_at(layer, b):
+            at = lax.div(b * n_slots, n_blocks)
+            prev = lax.div(b * n_slots - n_slots + n_blocks, n_blocks) - 1
+            t = layer * per_layer + far + 1 + lax.div(at, 4)
+            for k in range(4):
+                @pl.when((at != prev) & (lax.rem(at, 4) == k))
+                def _():
+                    slot(t, k)
 
         def loads(s, slot, down):
             if not down:
@@ -197,12 +207,11 @@
             if d < far:
                 same(v_hi, p_dsend, p_drecv, sib).start()
 
-        for t in range(far):
-            p_hop(t + 1)
-            tick_z(t)
-            tick_d(t)
-        tick_z(far)
-        tick_d(far)
+        for t in range(far + 1):
+            if t < far:
+                p_hop(t + 1)
+            for k in range(4):
+                slot(t, k)
 
         p_all = pg.at[:, 1 - core]
         same(p_all, p_dsend, p_drecv, sib).wait_recv()
@@ -225,10 +234,10 @@
                 c0 = (b % n_z) * lanes
                 tab[layer, 4 + b // n_z:5 + b // n_z, c0:c0 + lanes] = jnp.where(low[0:1], two[0], two[1])
 
-        def norms(layer):
-            @pl.loop(0, tokens // 64)
+        def norms(layer, r):
+            @pl.loop(0, blk // 64)
             def _(t):
-                rows = pl.ds(pl.multiple_of(t * 64, 64), 64)
+                rows = pl.ds(pl.multiple_of(r * blk + t * 64, 64), 64)
                 xf = x_s[rows, :].astype(F32)
                 mean = jnp.mean(xf, axis=-1, keepdims=True)
                 cen = xf - mean
@@ -309,117 +318,100 @@
             return pltpu.make_async_copy(x_s.at[:, cols], out_hbm.at[:, cols], out_sem.at[j])
 
         x_copy.wait()
-        norms(0)
-        fetch(0, 0)
 
         @pl.loop(0, n_layers)
         def _(layer):
             s0 = layer * per_layer
-            t0 = s0 + far + 1
+
+            @pl.loop(0, BLOCKS)
+            def _(r):
+                slots_at(layer, r)
+
+                @pl.when(r == 1)
+                def _():
+                    fetch(s0, 0)
+
+                norms(layer, r)
 
             @pl.loop(0, 3)
             def _(j):
-                slot = lax.rem(j, 2)
+                buf = lax.rem(j, 2)
 
                 @pl.loop(0, BLOCKS)
                 def _(r):
+                    slots_at(layer, BLOCKS * (j + 1) + r)
+
                     @pl.when(r == 0)
                     def _():
-                        tick_z(t0 + j)
-                        loads(s0 + j, slot, False)[0].wait()
-
-                    @pl.when(r == 2)
-                    def _():
-                        tick_d(t0 + j)
-
-                    qkv_block(layer, j, slot, r)
-
-                    @pl.when(r == BLOCKS - 1)
-                    def _():
-                        fetch(s0 + j + 1, 1 - slot)
+                        loads(s0 + j, buf, False)[0].wait()
+
+                    @pl.when(r == 1)
+                    def _():
+                        fetch(s0 + j + 1, 1 - buf)
+
+                    qkv_block(layer, j, buf, r)
 
             @pl.loop(0, docs)
             def _(n):
-                t = t0 + 3 + lax.div(n, docs // 2)
-
-                @pl.when(lax.rem(n, docs // 2) == 0)
+                slots_at(layer, 4 * BLOCKS + n)
+
+                @pl.when(n == docs - 2)
                 def _():
-                    tick_z(t)
-
-                @pl.when(lax.rem(n, docs // 2) == 2)
-                def _():
-                    tick_d(t)
+                    fetch(s0 + 4, 0)
 
                 attend(n)
 
             loads(s0 + 3, 1, False)[0].wait()
-            fetch(s0 + 4, 0)
 
             @pl.loop(0, BLOCKS)
             def _(r):
+                slots_at(layer, 4 * BLOCKS + docs + r)
                 out_block(layer, 1, r)
 
             @pl.loop(0, n_up)
             def _(j):
-                slot = lax.rem(j, 2)
+                buf = lax.rem(j, 2)
 
                 @pl.loop(0, BLOCKS)
                 def _(r):
+                    slots_at(layer, (5 + j) * BLOCKS + docs + r)
+
                     @pl.when(r == 0)
                     def _():
-                        tick_z(t0 + 5 + j)
-                        loads(s0 + 4 + j, slot, False)[0].wait()
-
-                    @pl.when(r == 2)
-                    def _():
-                        tick_d(t0 + 5 + j)
-
-                    up_block(layer, j, slot, r)
-
-                    @pl.when((r == BLOCKS - 1) & (j < n_up - 1))
-                    def _():
-                        fetch(s0 + 5 + j, 1 - slot)
-
-                    @pl.when((r == BLOCKS - 1) & (j == n_up - 1))
+                        loads(s0 + 4 + j, buf, False)[0].wait()
+
+                    @pl.when((r == 1) & (j < n_up - 1))
+                    def _():
+                        fetch(s0 + 5 + j, 1 - buf)
+
+                    @pl.when((r == 1) & (j == n_up - 1))
                     def _():
                         fetch(s0 + 4 + n_up, 0, True)
+
+                    up_block(layer, j, buf, r)
 
             @pl.loop(0, n_up)
             def _(j):
-                slot = lax.rem(j, 2)
+                buf = lax.rem(j, 2)
 
                 @pl.loop(0, BLOCKS)
                 def _(r):
-                    @pl.when((r == 0) & (j < n_up - 1))
-                    def _():
-                        tick_z(t0 + 5 + n_up + j)
+                    slots_at(layer, (5 + n_up + j) * BLOCKS + docs + r)
 
                     @pl.when(r == 0)
                     def _():
-                        for cp in loads(s0 + 4 + n_up + j, slot, True):
+                        for cp in loads(s0 + 4 + n_up + j, buf, True):
                             cp.wait()
 
-                    @pl.when((r == 2) & (j < n_up - 1))
-                    def _():
-                        tick_d(t0 + 5 + n_up + j)
-
-                    down_block(layer, j, slot, r)
-
-                    @pl.when((r == BLOCKS - 1) & (j < n_up - 1))
-                    def _():
-                        fetch(s0 + 5 + n_up + j, 1 - slot, True)
-
-                    @pl.when((r == BLOCKS - 1) & (j == n_up - 1) & (layer < n_layers - 1))
-                    def _():
-                        fetch(s0 + per_layer, 0)
+                    @pl.when((r == 1) & (j < n_up - 1))
+                    def _():
+                        fetch(s0 + 5 + n_up + j, 1 - buf, True)
+
+                    down_block(layer, j, buf, r)
 
                 @pl.when(layer == n_layers - 1)
                 def _():
                     out_copy(j).start()
-
-            @pl.when(layer < n_layers - 1)
-            def _():
-                norms(layer + 1)
 
         @pl.loop(0, n_st)
         def _(s):

time: 203 us -> 187 us (0.921)
  Pallas kernels: 191 us -> 176 us
    pallas_call x1, Pallas kernels: 191 us -> 176 us  [local_step(): call(hidden.reshape(docs * seq_len, d_model), lens, small, rope, wq, w_ou...]
where the time goes in v3:
time: 187 us
  Pallas kernels  176 us (94%)
  local copies, waits for them, and re-layouts  7.39 us (4%)
  other arithmetic  2.76 us (1%)
    pallas_call x1, Pallas kernels, local_step(): call(hidden.reshape(docs * seq_len, d_model), lens, small, rope, wq, w_ou...  176 us

profile of v3, /device:TPU:21, one launch (start us, length us, event | category | flops | bytes accessed | tf_op | source)
XLA Modules:
  0.0 186.6 jit_solution(14544859282344456315)
XLA Ops:
  0.0 0.7 bitcast_convert_fusion.1
  0.7 0.7 bitcast_convert_fusion
  1.3 0.7 reshape.37
  2.0 0.8 reshape.33
  2.8 1.4 select_maximum_fusion
  4.2 2.9 %reshape.30.wq_hbm = bf16[2,64,3072]{2,1,0:T(8,128)(2,1)} reshape(bf16[2,64,16,192]{3,2,1,0:T(8,128)(2,1)} %param.15) | data formatting | bytes 1572864 | tf_op jit(solution)/shard_map/reshape | solution.py:475
  7.1 176.4 %layers.1 = (bf16[1024,1024]{1,0:T(8,128)(2,1)}, bf16[24,8,2,64,1024]{4,3,2,1,0:T(8,128)(2,1)}) custom-call(bf16[1024,1024]{1,0:T(8,128)(2,1)} %bitcast.13, s32[8]{0:T(128)} %lens_ref.1, f32[32,128]{1,0:T(8,128)} %bitcast.15, f32[3,128,128]{2,1,0:T(8,128)} %constant.5.clone.rope_ref, bf16[2,64,3072]{2,1,0:T(8,128)(2,1)} %reshape.30.wq_hbm, ...), custom_call_target="tpu_custom_call" | custom-call | tf_op jit(solution)/shard_map/layers/pallas_call | solution.py:483
  183.5 3.1 %copy.18 = bf16[8,128,1024]{2,1,0:T(8,128)(2,1)} copy(bf16[8,128,1024]{2,1,0:T(8,128)(2,1)} %bitcast.14) | data formatting | bytes 4194304

commit v4 on v3

--- a/solution.py
+++ b/solution.py
@@ -52,9 +52,9 @@
     n_slots = 4 * per_layer
     n_blocks = BLOCKS * (5 + 2 * n_up) + docs
 
-    def kernel(x_hbm, lens_ref, par_ref, rope_ref, wq_hbm, wo_hbm, wu_hbm, wd_hbm,
+    def kernel(x_hbm, lens_ref, ln_ref, bq_ref, bo_ref, bu_ref, bd_ref, rope_ref, wq_hbm, wo_hbm, wu_hbm, wd_hbm,
                out_hbm, g,
-               x_s, a_s, m_s, qkv_s, ctx_s, act_s, acc_s, w_s, wd_s, st_q, st_o, st_u, st_d,
+               par_ref, x_s, a_s, m_s, q_r, k_r, v_r, qkv_s, ctx_s, act_s, acc_s, w_s, wd_s, st_q, st_o, st_u, st_d,
                pg, tab, tab_up,
                z_send, c_send, d_send, z_recv, x_recv, y_recv, d_recv,
                p_zsend, p_dsend, p_zrecv, p_drecv,
@@ -163,6 +163,23 @@
         for cp in st:
             cp.start()
         x_copy.start()
+
+        def twice(v):
+            return jnp.concatenate([v, v], axis=1)
+
+        for layer in range(n_layers):
+            r0 = layer * PAR_ROWS
+            row = slice(layer, layer + 1)
+            par_ref[r0:r0 + 4, :] = twice(ln_ref[layer])
+            b_q = bq_ref[row, :].astype(F32)
+            for j in range(3):
+                par_ref[r0 + 4 + j:r0 + 5 + j, :] = twice(b_q[:, j * head_dim:(j + 1) * head_dim])
+            par_ref[r0 + 7:r0 + 8, :] = twice(bo_ref[row, :].astype(F32))
+            par_ref[r0 + 8:r0 + 9, :] = twice(bd_ref[row, :].astype(F32))
+            for j in range(down_rows // lanes):
+                par_ref[r0 + 9 + j:r0 + 10 + j, :] = bu_ref[row, j * lanes:(j + 1) * lanes].astype(F32)
+            r1 = 9 + down_rows // lanes
+            par_ref[r0 + r1:r0 + PAR_ROWS, :] = jnp.zeros((PAR_ROWS - r1, lanes), F32)
         barrier = pltpu.get_barrier_semaphore()
         for dev in (up_z, dn_z, x_dev, y_dev, sib):
             pl.semaphore_signal(barrier, inc=1, device_id=dev, device_id_type=MESH)
@@ -270,7 +287,6 @@
             zero = jnp.zeros((seq_len, lanes), BF)
 
             def rope(v):
-                v = v.astype(F32)
                 return (v * rope_ref[0] + pltpu.roll(v, lanes - half_rot, 1) * rope_ref[1]
                         + pltpu.roll(v, half_rot, 1) * rope_ref[2]).astype(BF)
 
@@ -279,16 +295,20 @@
                 trio = []
                 for b in range(3 * p, 3 * p + 3):
                     trio.append(qkv_s[b // n_z, rows, (b % n_z) * lanes:(b % n_z + 1) * lanes])
-                q2 = rope(jnp.where(first, trio[0], trio[1]))
-                k2 = rope(pltpu.roll(jnp.where(first, trio[2], trio[0]).astype(F32), head_dim, 1))
-                v2 = jnp.where(first, trio[1], trio[2])
+                q_r[:, cs] = rope(jnp.where(first, trio[0], trio[1]).astype(F32))
+                k_r[:, cs] = rope(pltpu.roll(jnp.where(first, trio[2], trio[0]).astype(F32), head_dim, 1))
+                v_r[:, cs] = jnp.where(first, trio[1], trio[2])
+
+            for p in range(n_heads // 2):
+                cs = slice(p * lanes, (p + 1) * lanes)
+                k2, v2 = k_r[:, cs], v_r[:, cs]
                 kk = jnp.concatenate([jnp.where(first, k2, zero), jnp.where(first, zero, k2)], axis=0)
                 vv = jnp.concatenate([jnp.where(first, v2, zero), jnp.where(first, zero, v2)], axis=0)
-                sc = lax.dot_general(q2, kk, (((1,), (1,)), ((), ())), preferred_element_type=F32)
+                sc = lax.dot_general(q_r[:, cs], kk, (((1,), (1,)), ((), ())), preferred_element_type=F32)
                 probs = []
                 for j in range(2):
-                    s1 = jnp.where(vis, sc[:, j * seq_len:(j + 1) * seq_len] * (head_dim ** -0.5), -1e30)
-                    e = jnp.exp(s1 - jnp.max(s1, axis=-1, keepdims=True))
+                    s1 = jnp.where(vis, sc[:, j * seq_len:(j + 1) * seq_len] * (head_dim ** -0.5 * math.log2(math.e)), -1e30)
+                    e = jnp.exp2(s1 - jnp.max(s1, axis=-1, keepdims=True))
                     probs.append((e * (1.0 / jnp.sum(e, axis=-1, keepdims=True))).astype(BF))
                 ctx_s[rows, cs] = dot(jnp.concatenate(probs, axis=1), vv).astype(BF)
 
@@ -434,8 +454,9 @@
     dma = pltpu.SemaphoreType.DMA
     n_own = n_layers * (4 + n_up + n_up * parts)
     act = pltpu.VMEM((tokens, d_model), BF)
+    doc_v = pltpu.VMEM((seq_len, d_model), BF)
     scratch = [
-        act, act, act, pltpu.VMEM((3, tokens, d_model), BF), act, pltpu.VMEM((tokens, ff), BF),
+        pltpu.VMEM((n_layers * PAR_ROWS, lanes), F32), act, act, act, doc_v, doc_v, doc_v, pltpu.VMEM((3, tokens, d_model), BF), act, pltpu.VMEM((tokens, ff), BF),
         pltpu.VMEM((tokens, d_model), F32),
         pltpu.VMEM((2, n_z, 2, rows_w, d_model), BF), pltpu.VMEM((2, n_z, 2, down_rows, d_cols), BF),
         pltpu.VMEM((n_layers, rows_w, 3 * d_model), BF), pltpu.VMEM((n_layers, rows_w, d_model), BF),
@@ -454,7 +475,7 @@
         kernel,
         name="layers",
         out_shape=out_shape,
-        in_specs=[hbm, smem, vmem, vmem, hbm, hbm, hbm, hbm],
+        in_specs=[hbm, smem] + [vmem] * 6 + [hbm] * 4,
         out_specs=(hbm, hbm),
         scratch_shapes=scratch,
         compiler_params=pltpu.CompilerParams(collective_id=0, has_side_effects=True, vmem_limit_bytes=67043328),
@@ -473,14 +494,9 @@
         head_dim = triple // 3
         ff = w_up.shape[2]
         wq = w_qkv.reshape(n_layers, rows, n_heads * triple)
-        small = jnp.concatenate([ln_par, b_qkv.astype(F32).reshape(n_layers, 3, -1), b_out.astype(F32)[:, None],
-                                 b_down.astype(F32)[:, None]], axis=1)
-        small = jnp.concatenate([small, small], axis=2)
-        small = jnp.concatenate([small, b_up.astype(F32).reshape(n_layers, -1, 2 * head_dim)], axis=1)
-        small = jnp.pad(small, ((0, 0), (0, PAR_ROWS - small.shape[1]), (0, 0))).reshape(-1, 2 * head_dim)
-        rope = jnp.asarray(rotary_lanes(seq_len, head_dim))
         call = make_kernel(n_layers, n_z, side, docs, seq_len, d_model, n_heads, ff)
-        out = call(hidden.reshape(docs * seq_len, d_model), lens, small, rope, wq, w_out, w_up, w_down)[0]
+        out = call(hidden.reshape(docs * seq_len, d_model), lens, ln_par, b_qkv, b_out, b_up, b_down, jnp.asarray(rotary_lanes(seq_len, head_dim)),
+                   wq, w_out, w_up, w_down)[0]
         return out.reshape(docs, seq_len, d_model)
 
     return jax.shard_map(local_step, mesh=mesh, in_specs=in_specs, out_specs=row_spec, check_vma=False)

time: 187 us -> 183 us (0.979)
  other arithmetic: 2.76 us -> 0 us
where the time goes in v4:
time: 183 us
  Pallas kernels  177 us (97%)
  local copies, waits for them, and re-layouts  5.94 us (3%)
    pallas_call x1, Pallas kernels, local_step(): call(hidden.reshape(docs * seq_len, d_model), lens, ln_par, b_qkv, b_out,...  177 us

profile of v4, /device:TPU:21, one launch (start us, length us, event | category | flops | bytes accessed | tf_op | source)
XLA Modules:
  0.0 182.8 jit_solution(18277674242652213296)
XLA Ops:
  0.0 2.9 %reshape.10.wq_hbm = bf16[2,64,3072]{2,1,0:T(8,128)(2,1)} reshape(bf16[2,64,16,192]{3,2,1,0:T(8,128)(2,1)} %param.15) | data formatting | bytes 1572864 | tf_op jit(solution)/shard_map/reshape | solution.py:496
  2.9 176.9 %layers.1 = (bf16[1024,1024]{1,0:T(8,128)(2,1)}, bf16[24,8,2,64,1024]{4,3,2,1,0:T(8,128)(2,1)}) custom-call(bf16[1024,1024]{1,0:T(8,128)(2,1)} %bitcast.4, s32[8]{0:T(128)} %lens_ref.1, f32[2,4,64]{2,1,0:T(4,128)} %ln_ref.1, bf16[2,192]{1,0:T(2,128)(2,1)} %bq_ref.1, bf16[2,64]{1,0:T(2,128)(2,1)} %bo_ref.1, bf16[2,256]{1,0:T(2,128)(2,1)} %bu_ref.1, ...), custom_call_target="tpu_custom_call" | custom-call | tf_op jit(solution)/shard_map/layers/pallas_call | solution.py:498
  179.8 3.1 %copy.14 = bf16[8,128,1024]{2,1,0:T(8,128)(2,1)} copy(bf16[8,128,1024]{2,1,0:T(8,128)(2,1)} %bitcast.5) | data formatting | bytes 4194304

commit v5 on v4

--- a/solution.py
+++ b/solution.py
@@ -24,13 +24,13 @@
     inv_freq = (1.0 / (ROPE_BASE ** (np.arange(0, rot, 2, dtype=np.float32) / rot))).astype(np.float32)
     angles = np.arange(seq_len, dtype=np.float32)[:, None] * inv_freq[None, :]
     cos_v, sin_v = np.cos(angles), np.sin(angles)
-    tab = np.zeros((3, seq_len, 2 * head_dim), np.float32)
+    tab = np.zeros((2, seq_len, 2 * head_dim), np.float32)
     tab[0] = 1.0
     for base in (0, head_dim):
         tab[0, :, base:base + half] = cos_v
         tab[0, :, base + half:base + rot] = cos_v
         tab[1, :, base:base + half] = -sin_v
-        tab[2, :, base + half:base + rot] = sin_v
+        tab[1, :, base + half:base + rot] = sin_v
     return tab
 
 
@@ -282,35 +282,38 @@
             rows = pl.ds(pl.multiple_of(n * seq_len, seq_len), seq_len)
             pos_q = lax.broadcasted_iota(jnp.int32, (seq_len, seq_len), 0)
             pos_k = lax.broadcasted_iota(jnp.int32, (seq_len, seq_len), 1)
-            vis = pos_k <= jnp.minimum(pos_q, lens_ref[n] - 1)
-            first = lax.broadcasted_iota(jnp.int32, (seq_len, lanes), 1) < head_dim
+            vis = pos_q <= jnp.minimum(pos_k, lens_ref[n] - 1)
+            lane = lax.broadcasted_iota(jnp.int32, (seq_len, lanes), 1)
+            first = lane < head_dim
+            front = lax.rem(lane, 2 * half_rot) < half_rot
             zero = jnp.zeros((seq_len, lanes), BF)
 
-            def rope(v):
-                return (v * rope_ref[0] + pltpu.roll(v, lanes - half_rot, 1) * rope_ref[1]
-                        + pltpu.roll(v, half_rot, 1) * rope_ref[2]).astype(BF)
+            def rope(u, turn):
+                v = pltpu.roll(u, turn, 1) if turn else u
+                moved = jnp.where(front, pltpu.roll(u, (turn - half_rot) % lanes, 1), pltpu.roll(u, turn + half_rot, 1))
+                return (v.astype(F32) * rope_ref[0] + moved.astype(F32) * rope_ref[1]).astype(BF)
 
             for p in range(n_heads // 2):
                 cs = slice(p * lanes, (p + 1) * lanes)
                 trio = []
                 for b in range(3 * p, 3 * p + 3):
                     trio.append(qkv_s[b // n_z, rows, (b % n_z) * lanes:(b % n_z + 1) * lanes])
-                q_r[:, cs] = rope(jnp.where(first, trio[0], trio[1]).astype(F32))
-                k_r[:, cs] = rope(pltpu.roll(jnp.where(first, trio[2], trio[0]).astype(F32), head_dim, 1))
+                q_r[:, cs] = rope(jnp.where(first, trio[0], trio[1]), 0)
+                k_r[:, cs] = rope(jnp.where(first, trio[2], trio[0]), head_dim)
                 v_r[:, cs] = jnp.where(first, trio[1], trio[2])
 
             for p in range(n_heads // 2):
                 cs = slice(p * lanes, (p + 1) * lanes)
-                k2, v2 = k_r[:, cs], v_r[:, cs]
-                kk = jnp.concatenate([jnp.where(first, k2, zero), jnp.where(first, zero, k2)], axis=0)
-                vv = jnp.concatenate([jnp.where(first, v2, zero), jnp.where(first, zero, v2)], axis=0)
-                sc = lax.dot_general(q_r[:, cs], kk, (((1,), (1,)), ((), ())), preferred_element_type=F32)
-                probs = []
-                for j in range(2):
+                q2, v2 = q_r[:, cs], v_r[:, cs]
+                qq = jnp.concatenate([jnp.where(first, q2, zero), jnp.where(first, zero, q2)], axis=0)
+                sc = lax.dot_general(k_r[:, cs], qq, (((1,), (1,)), ((), ())), preferred_element_type=F32)
+                ctx = []
+                for j, vj in enumerate((jnp.where(first, v2, zero), jnp.where(first, zero, v2))):
                     s1 = jnp.where(vis, sc[:, j * seq_len:(j + 1) * seq_len] * (head_dim ** -0.5 * math.log2(math.e)), -1e30)
-                    e = jnp.exp2(s1 - jnp.max(s1, axis=-1, keepdims=True))
-                    probs.append((e * (1.0 / jnp.sum(e, axis=-1, keepdims=True))).astype(BF))
-                ctx_s[rows, cs] = dot(jnp.concatenate(probs, axis=1), vv).astype(BF)
+                    e = jnp.exp2(s1 - jnp.max(s1, axis=0, keepdims=True))
+                    pr = (e * (1.0 / jnp.sum(e, axis=0, keepdims=True))).astype(BF)
+                    ctx.append(lax.dot_general(pr, vj, (((0,), (0,)), ((), ())), preferred_element_type=F32))
+                ctx_s[rows, cs] = (ctx[0] + ctx[1]).astype(BF)
 
         def out_block(layer, slot, r):
             rows = rows_of(r)

time: 183 us -> 172 us (0.940)
  Pallas kernels: 177 us -> 166 us
    pallas_call x1, Pallas kernels: 177 us -> 166 us  [local_step(): call(hidden.reshape(docs * seq_len, d_model), lens, ln_par, b_qkv, b_out,...]
where the time goes in v5:
time: 172 us
  Pallas kernels  166 us (97%)
  local copies, waits for them, and re-layouts  5.94 us (3%)
    pallas_call x1, Pallas kernels, local_step(): call(hidden.reshape(docs * seq_len, d_model), lens, ln_par, b_qkv, b_out,...  166 us

profile of v5, /device:TPU:21, one launch (start us, length us, event | category | flops | bytes accessed | tf_op | source)
XLA Modules:
  0.0 172.1 jit_solution(6637946291468731083)
XLA Ops:
  0.0 2.9 %reshape.10.wq_hbm = bf16[2,64,3072]{2,1,0:T(8,128)(2,1)} reshape(bf16[2,64,16,192]{3,2,1,0:T(8,128)(2,1)} %param.15) | data formatting | bytes 1572864 | tf_op jit(solution)/shard_map/reshape | solution.py:499
  2.9 166.1 %layers.1 = (bf16[1024,1024]{1,0:T(8,128)(2,1)}, bf16[24,8,2,64,1024]{4,3,2,1,0:T(8,128)(2,1)}) custom-call(bf16[1024,1024]{1,0:T(8,128)(2,1)} %bitcast.4, s32[8]{0:T(128)} %lens_ref.1, f32[2,4,64]{2,1,0:T(4,128)} %ln_ref.1, bf16[2,192]{1,0:T(2,128)(2,1)} %bq_ref.1, bf16[2,64]{1,0:T(2,128)(2,1)} %bo_ref.1, bf16[2,256]{1,0:T(2,128)(2,1)} %bu_ref.1, ...), custom_call_target="tpu_custom_call" | custom-call | tf_op jit(solution)/shard_map/layers/pallas_call | solution.py:501
  169.0 3.1 %copy.14 = bf16[8,128,1024]{2,1,0:T(8,128)(2,1)} copy(bf16[8,128,1024]{2,1,0:T(8,128)(2,1)} %bitcast.5) | data formatting | bytes 4194304
